TPU v7x, 256 devices: a whole 4x4x8 slice. The times are simulated.
256 devices in a mesh: rep: 2 (over core), dp: 128 (over x, y, z).
Axes of the slice: x: 4, y: 4, z: 8, core: 2. Of those that a mesh axis runs over, the one named last changes fastest.
Arguments:
- x: bfloat16 [256, 1024, 512], P(('rep', 'dp')), parts along dimension 0
- dy: bfloat16 [256, 1024, 512], P(('rep', 'dp')), parts along dimension 0
- w_gate: bfloat16 [2, 512, 8192], replicated
- w_up: bfloat16 [2, 512, 8192], replicated
- w_down: bfloat16 [2, 8192, 512], replicated
- m_w_gate: float32 [2, 512, 8192], P(None, 'dp')
- m_w_up: float32 [2, 512, 8192], P(None, 'dp')
- m_w_down: float32 [2, 8192, 512], P(None, 'dp')
- v_w_gate: float32 [2, 512, 8192], P(None, 'dp')
- v_w_up: float32 [2, 512, 8192], P(None, 'dp')
- v_w_down: float32 [2, 8192, 512], P(None, 'dp')
Outputs:
- output 1: bfloat16 [4, 512, 8192], P('rep'), parts along dimension 0
- output 2: bfloat16 [4, 512, 8192], P('rep'), parts along dimension 0
- output 3: bfloat16 [4, 8192, 512], P('rep'), parts along dimension 0
- output 4: float32 [4, 512, 8192], P('rep', 'dp'), parts along dimension 0
- output 5: float32 [4, 512, 8192], P('rep', 'dp'), parts along dimension 0
- output 6: float32 [4, 8192, 512], P('rep', 'dp'), parts along dimension 0
- output 7: float32 [4, 512, 8192], P('rep', 'dp'), parts along dimension 0
- output 8: float32 [4, 512, 8192], P('rep', 'dp'), parts along dimension 0
- output 9: float32 [4, 8192, 512], P('rep', 'dp'), parts along dimension 0
There are 2 independent parts. A program takes and returns all parts, laid end to end along the dimension named above; an argument that names none is the same for every part.
All inputs are finite; a program needn't handle non-finite values.
Results may differ from a plain program's by a relative error of at most 0.022.
Values are sent between devices in bfloat16 or wider.
A program may use at most 768 MiB of HBM per device.

v0:
```python
import jax
import jax.numpy as jnp
from jax import lax

NAMES = ("w_gate", "w_up", "w_down")


def matmul(a, w):
    return jnp.dot(a, w, preferred_element_type=jnp.float32).astype(jnp.bfloat16)


def normed(h):
    wide = h.astype(jnp.float32)
    scale = lax.rsqrt(jnp.mean(wide**2, -1, keepdims=True) + 1e-6)
    return (wide * scale).astype(jnp.bfloat16)


def layer(h, w):
    a = normed(h)
    gate = jnp.dot(a, w["w_gate"], preferred_element_type=jnp.float32)
    up = jnp.dot(a, w["w_up"], preferred_element_type=jnp.float32)
    return h + matmul((jax.nn.silu(gate) * up).astype(jnp.bfloat16), w["w_down"])


def adamw(w, m, v, g):
    m = 0.9 * m + 0.1 * g
    v = 0.95 * v + 0.05 * g * g
    step = m * lax.rsqrt(v + 1e-8) + 0.1 * w
    return (w - 0.02 * step).astype(jnp.bfloat16), m, v


def stack(weights, h):
    for number in range(weights["w_gate"].shape[0]):
        h = layer(h, {name: w[number] for name, w in weights.items()})
    return h


def solution(mesh):
    groups = mesh.shape["rep"]

    def step(x, dy, *arrays):
        weights, m, v = (arrays[i : i + 3] for i in (0, 3, 6))
        x, dy = (t.reshape(groups, -1, *t.shape[1:]) for t in (x, dy))

        def of_a_group(x, dy):
            _, back = jax.vjp(lambda w: stack(w, x), dict(zip(NAMES, weights, strict=True)))
            by_weights = back(dy)[0]
            gradients = [by_weights[name].astype(jnp.float32) for name in NAMES]
            new = [adamw(w.astype(jnp.float32), m, v, g) for w, m, v, g in zip(weights, m, v, gradients, strict=True)]
            return tuple(one[which] for which in range(3) for one in new)

        return tuple(t.reshape(-1, *t.shape[2:]) for t in jax.vmap(of_a_group)(x, dy))

    return step
```

profile of v0, /device:TPU:2, one launch (start us, length us, event | category | flops | bytes accessed | tf_op | source)
XLA Modules:
  0.0 2897.7 jit_solution(13997234606333876712)
XLA Ops:
  7.2 0.0 reduce-scatter.17.cloned.1.call-start
  7.2 1.5 fusion.71
  8.7 1.5 copy.2
  10.3 19.3 fusion.60
  29.6 17.9 fusion.58
  47.5 27.4 fusion.26
  74.9 14.9 fusion.75
  89.9 19.1 fusion.49
  109.1 18.8 fusion.52
  127.9 15.2 convolution_convert_fusion.1
  143.1 0.5 copy.3
  143.6 33.4 %fusion.6 = bf16[1024,8192]{1,0:T(8,128)(2,1)} fusion(f32[1024,8192]{1,0:T(8,128)} %fusion.49, f32[1024,8192]{1,0:T(8,128)} %fusion.52, bf16[1024,8192]{1,0:T(8,128)(2,1)} %convolution_convert_fusion.1), kind=kLoop, calls=%fused_computation.11 | loop fusion | flops 100663296 | bytes 100663296
  177.0 15.7 fusion.81
  192.7 24.3 fusion.77
  217.1 1.9 fusion.108
  219.0 1.0 copy-done.8
  220.0 16.0 convolution_bitcast_fusion
  236.0 0.0 reduce-scatter.17.cloned.1.call-update
  236.0 0.0 reduce-scatter.15.cloned.1.call-start
  236.0 29.5 %fusion.35 = f32[1,8192,512]{2,1,0:T(8,128)} fusion(f32[1024,8192]{1,0:T(8,128)} %fusion.52, f32[1024,8192]{1,0:T(8,128)} %fusion.49, bf16[1,1024,512]{2,1,0:T(8,128)(2,1)S(1)} %copy-done.5), kind=kOutput, calls=%fused_computation.45 | convolution fusion | flops 8640266240 | bytes 84934656 | tf_op jit(solution)/vmap(transpose(jvp()))/dot_general | solution.py:9
  265.5 0.0 all-gather.12.cloned.1.call-start
  265.6 1.1 copy-done.9
  266.7 16.3 convolution_convert_fusion
  283.0 0.6 fusion.156
  284.3 25.6 fusion.44
  309.9 36.1 %fusion.41 = f32[1,512,8192]{2,1,0:T(8,128)} fusion(f32[1024,8192]{1,0:T(8,128)} %fusion.60, f32[1024,8192]{1,0:T(8,128)} %fusion.58, bf16[1024,8192]{1,0:T(8,128)(2,1)} %convolution_convert_fusion, bf16[1,1024,512]{1,2,0:T(8,128)(2,1)S(1)} %copy-done.7, f32[1024]{0:T(1024)S(1)} %copy-done.17), kind=kOutput, calls=%fused_computation.47 | convolution fusion | flops 8683782144 | bytes 101715968 | tf_op jit(solution)/vmap(transpose(jvp()))/dot_general | solution.py:20
  346.0 15.8 convolution_bitcast_fusion.1
  361.8 25.7 fusion.38
  388.2 1969.8 %all-reduce.12 = (bf16[1,512,8192]{2,1,0:T(8,128)(2,1)}, bf16[1,512,8192]{2,1,0:T(8,128)(2,1)}, bf16[1,512,8192]{2,1,0:T(8,128)(2,1)}, bf16[1,512,8192]{2,1,0:T(8,128)(2,1)}) all-reduce(f32[1,512,8192]{2,1,0:T(8,128)} %fusion.41, f32[1,512,8192]{2,1,0:T(8,128)} %convolution_bitcast_fusion.1, ...), channel_id=14, replica_groups=[2,128]<=[256], use_global_device_ids=true, to_apply=%add.1.clone.clone | all-reduce | flops 16777216 | bytes 100663296
  2358.0 1.0 fusion.149
  2359.1 2.1 fusion.145
  2361.1 0.8 copy.5
  2362.0 0.0 all-gather.10.cloned.1.call-start
  2362.0 1.0 fusion.147
  2363.1 2.1 fusion.146
  2365.2 0.8 copy.4
  2366.0 0.0 all-gather.14.cloned.1.call-start
  2366.0 0.0 reduce-scatter.17.cloned.1.call-done
  2366.1 0.9 convert_bitcast_fusion.3
  2367.0 0.0 reduce-scatter.15.cloned.1.call-done
  2367.0 0.9 convert_bitcast_fusion.4
  2367.9 1.9 fusion.142
  2369.8 204.4 %all-gather.12.cloned.1.call-done = bf16[1,2,512,8192]{3,1,0,2:T(2,128)(2,1)} async-done(((bf16[1,2,4,8192]{3,1,0,2:T(2,128)(2,1)}), bf16[1,2,512,8192]{3,1,0,2:T(2,128)(2,1)}) %all-gather.12.cloned.1.call-update) | async-done | bytes 16777232 | tf_op jit(solution)/reshape | solution.py:52
  2574.3 18.5 copy.7
  2592.8 132.8 %all-gather.10.cloned.1.call-done = bf16[1,2,512,8192]{3,1,0,2:T(2,128)(2,1)} async-done(((bf16[1,2,4,8192]{3,1,0,2:T(2,128)(2,1)}), bf16[1,2,512,8192]{3,1,0,2:T(2,128)(2,1)}) %all-gather.10.cloned.1.call-update) | async-done | bytes 16777232 | tf_op jit(solution)/reshape | solution.py:52
  2725.6 18.5 copy.6
  2744.1 132.7 %all-gather.14.cloned.1.call-done = bf16[1,2,8192,512]{3,2,1,0:T(8,128)(2,1)} async-done(((bf16[1,2,64,512]{3,2,1,0:T(8,128)(2,1)}), bf16[1,2,8192,512]{3,2,1,0:T(8,128)(2,1)}) %all-gather.14.cloned.1.call-update) | async-done | bytes 16777232 | tf_op jit(solution)/reshape | solution.py:52
  2876.8 13.8 copy.25
  (44 shorter events, 0.2 us)
Async XLA Ops:
  7.2 2358.9 %reduce-scatter.17.cloned.1.call-start = ((), (), s32[]{:S(2)}) async-start(), calls=%async_computation.6 | async-start | bytes 16908288
  10.2 64.7 %copy-start.6 = (bf16[1,1024,512]{1,2,0:T(8,128)(2,1)}, bf16[1,1024,512]{1,2,0:T(8,128)(2,1)S(1)}, u32[]{:S(2)}) copy-start(bf16[1,1024,512]{1,2,0:T(8,128)(2,1)S(1)} %copy.2) | copy-start | bytes 3145732
  10.2 19.4 copy-start.16
  10.3 19.4 copy-start.2
  89.9 127.1 %copy-start = (bf16[1,1,1024,512]{2,3,1,0:T(8,128)(2,1)}, bf16[1,1,1024,512]{2,3,1,0:T(8,128)(2,1)S(1)}, u32[]{:S(2)}) copy-start(bf16[1,1,1024,512]{2,3,1,0:T(8,128)(2,1)S(1)} %get-tuple-element.25) | copy-start | bytes 3145732
  89.9 127.1 %copy-start.3 = (f32[1,1,1024]{2,1,0:T(1,128)}, f32[1,1,1024]{2,1,0:T(1,128)S(1)}, u32[]{:S(2)}) copy-start(f32[1,1,1024]{2,1,0:T(1,128)S(1)} %rsqrt.31) | copy-start | bytes 12292
  109.1 18.8 copy-start.5
  219.0 1.0 copy-start.8
  236.0 2131.0 %reduce-scatter.15.cloned.1.call-start = ((), (), s32[]{:S(2)}) async-start(), calls=%async_computation.5 | async-start | bytes 16908288
  265.5 1.2 copy-start.9
  265.5 2308.8 %all-gather.12.cloned.1.call-start = ((), (), s32[]{:S(2)}) async-start(), calls=%async_computation.3 | async-start | bytes 16908288 | tf_op jit(solution)/reshape | solution.py:52
  266.7 16.3 copy-start.18
  266.7 17.6 copy-start.7
  266.7 17.6 copy-start.17
  309.9 36.1 %copy-start.1 = (bf16[1,1,1024,512]{2,3,1,0:T(8,128)(2,1)S(1)}, bf16[1,1,1024,512]{2,3,1,0:T(8,128)(2,1)}, u32[]{:S(2)}) copy-start(bf16[1,1,1024,512]{2,3,1,0:T(8,128)(2,1)} %copy-done) | copy-start | bytes 3145732
  309.9 36.1 %copy-start.4 = (f32[1,1,1024]{2,1,0:T(1,128)S(1)}, f32[1,1,1024]{2,1,0:T(1,128)}, u32[]{:S(2)}) copy-start(f32[1,1,1024]{2,1,0:T(1,128)} %copy-done.3) | copy-start | bytes 12292
  388.1 1970.9 %copy-start.10 = (f32[2,4,8192]{2,1,0:T(4,128)S(1)}, f32[2,4,8192]{2,1,0:T(4,128)}, u32[]{:S(2)}) copy-start(f32[2,4,8192]{2,1,0:T(4,128)} %param.8) | copy-start | bytes 786436
  388.2 1970.9 %copy-start.11 = (f32[2,4,8192]{2,1,0:T(4,128)S(1)}, f32[2,4,8192]{2,1,0:T(4,128)}, u32[]{:S(2)}) copy-start(f32[2,4,8192]{2,1,0:T(4,128)} %param.7) | copy-start | bytes 786436
  388.2 1974.9 %copy-start.12 = (f32[2,4,8192]{2,1,0:T(4,128)S(1)}, f32[2,4,8192]{2,1,0:T(4,128)}, u32[]{:S(2)}) copy-start(f32[2,4,8192]{2,1,0:T(4,128)} %param.6) | copy-start | bytes 786436
  388.2 1974.9 %copy-start.13 = (f32[2,4,8192]{2,1,0:T(4,128)S(1)}, f32[2,4,8192]{2,1,0:T(4,128)}, u32[]{:S(2)}) copy-start(f32[2,4,8192]{2,1,0:T(4,128)} %param.1) | copy-start | bytes 786436
  388.2 1979.7 %copy-start.14 = (f32[2,64,512]{2,1,0:T(8,128)S(1)}, f32[2,64,512]{2,1,0:T(8,128)}, u32[]{:S(2)}) copy-start(f32[2,64,512]{2,1,0:T(8,128)} %param.10) | copy-start | bytes 786436
  388.2 1979.7 %copy-start.15 = (f32[2,64,512]{2,1,0:T(8,128)S(1)}, f32[2,64,512]{2,1,0:T(8,128)}, u32[]{:S(2)}) copy-start(f32[2,64,512]{2,1,0:T(8,128)} %param.9) | copy-start | bytes 786436
  2362.0 363.6 %all-gather.10.cloned.1.call-start = ((), (), s32[]{:S(2)}) async-start(), calls=%async_computation.2 | async-start | bytes 16908288 | tf_op jit(solution)/reshape | solution.py:52
  2366.0 510.9 %all-gather.14.cloned.1.call-start = ((), (), s32[]{:S(2)}) async-start(), calls=%async_computation.4 | async-start | bytes 16908288 | tf_op jit(solution)/reshape | solution.py:52
Sparse Core Ops, SparseCore 0:
  236.1 695.6 reduce-scatter.16
  934.3 778.0 reduce-scatter.14
  2362.1 212.1 all-gather.11
  2578.3 147.2 all-gather.9
  2729.0 147.8 all-gather.13
where the time goes:
time: 2910 us; the launch traced here: 2900 us
  blocking collectives  1970 us (68%)
  waiting for transfers between devices  470 us (16%)
  matrix products  310 us (11%)
  other arithmetic  72.1 us (2%)
  local copies, waits for them, and re-layouts  59.3 us (2%)
    unnamed x1, blocking collectives  1970 us
    reshape x3, waiting for transfers between devices, step(): t.reshape(-1, *t.shape[2:])  470 us
    dot_general x5, matrix products, layer(): up = jnp.dot(a, w['w_up'], preferred_element_type=jnp.float32)  112 us
    dot_general x5, matrix products, layer(): gate = jnp.dot(a, w['w_gate'], preferred_element_type=jnp.float32)  106 us
    dot_general x5, matrix products, matmul(): jnp.dot(a, w, preferred_element_type=jnp.float32).astype(jnp.bfloat16)  92 us
    unnamed x3, other arithmetic  62.7 us
  transfers between devices with their start and end apart: 5, of which 3 were waited for; matrix products, arithmetic and copies ran while one was open for 7% of the time, Pallas kernels for 0%

commit v1 on v0

v1 whole, which is shorter than its diff:
```python
import functools

import jax
import jax.numpy as jnp
from jax import lax
from jax.experimental import pallas as pl
from jax.experimental.pallas import tpu as pltpu
from jax.sharding import PartitionSpec as P

GRID = (4, 4, 8)
BF, F32 = jnp.bfloat16, jnp.float32
MESH = pl.DeviceIdType.MESH
VMEM_LIMIT = 66_000_000
LAG = 2
SLOTS = 6
JOBS = 4


def dot(a, b, dims=((1,), (0,))):
    return lax.dot_general(a, b, (dims, ((), ())), preferred_element_type=F32)


def normed(h):
    wide = h.astype(F32)
    scale = lax.rsqrt(jnp.mean(wide**2, -1, keepdims=True) + 1e-6)
    return (wide * scale).astype(BF)


def place():
    nx, ny, nz = GRID
    me = lax.axis_index("dp")
    at = (lax.div(me, ny * nz), lax.rem(lax.div(me, nz), ny), lax.rem(me, nz))

    def neighbour(axis, step):
        c = list(at)
        c[axis] = lax.rem(at[axis] + (step + GRID[axis]), GRID[axis])
        return (c[0] * ny + c[1]) * nz + c[2]

    return at, neighbour


def meet(neighbour):
    barrier = pltpu.get_barrier_semaphore()
    for axis in range(3):
        for step in (1, -1):
            pl.semaphore_signal(barrier, inc=1, device_id={"dp": neighbour(axis, step)}, device_id_type=MESH)
    pl.semaphore_wait(barrier, 6)


class Sender:
    def __init__(self, axis, at, neighbour, send, recv):
        self.n, self.p = GRID[axis], at[axis]
        self.to = (neighbour(axis, 1), neighbour(axis, -1))
        self.send, self.recv = send, recv

    def block(self, step):
        return lax.rem(self.p + (step + self.n), self.n)

    def copy(self, step, slot, d, src, dst):
        return pltpu.make_async_remote_copy(
            src_ref=src, dst_ref=dst, send_sem=self.send.at[step, slot, d], recv_sem=self.recv.at[step, slot, d],
            device_id={"dp": self.to[d]}, device_id_type=MESH,
        )

    def wait(self, step, slot, refs):
        for d in (0, 1):
            c = self.copy(step, slot, d, refs[d], refs[d])
            c.wait_recv()
            c.wait_send()


def forward_kernel(x_ref, wg, wu, wd, a_all, at_all, h1, acc):
    i = pl.program_id(0)

    @pl.when(i == 0)
    def _():
        a = normed(x_ref[...])
        a_all[0] = a
        at_all[0] = a.T
        acc[...] = jnp.zeros_like(acc)

    a = a_all[0]
    gate = dot(a, wg[0])
    up = dot(a, wu[0])
    hidden = (gate * jax.nn.sigmoid(gate) * up).astype(BF)
    acc[...] += dot(hidden, wd[0])

    @pl.when(i == pl.num_programs(0) - 1)
    def _():
        h = x_ref[...] + acc[...].astype(BF)
        h1[...] = h
        a = normed(h)
        a_all[1] = a
        at_all[1] = a.T


def forward(x, wg, wu, wd):
    (tokens, d), ff = x.shape, wg.shape[2]
    f = ff // 16
    return pl.pallas_call(
        forward_kernel,
        grid=(16,),
        in_specs=[
            pl.BlockSpec(memory_space=pltpu.VMEM),
            pl.BlockSpec((1, d, f), lambda i: (0, 0, i)),
            pl.BlockSpec((1, d, f), lambda i: (0, 0, i)),
            pl.BlockSpec((1, f, d), lambda i: (0, i, 0)),
        ],
        out_specs=[pl.BlockSpec(memory_space=pltpu.VMEM)] * 3,
        out_shape=[
            jax.ShapeDtypeStruct((2, tokens, d), BF),
            jax.ShapeDtypeStruct((2, d, tokens), BF),
            jax.ShapeDtypeStruct((tokens, d), BF),
        ],
        scratch_shapes=[pltpu.VMEM((tokens, d), F32)],
        compiler_params=pltpu.CompilerParams(vmem_limit_bytes=VMEM_LIMIT, dimension_semantics=("arbitrary",)),
        name="forward",
    )(x, wg, wu, wd)


def compute(layer, blocks, a_all, at_all, dh, wg, wu, wd, hid, dgate, dup, da):
    tokens = dgate.shape[0]
    rows = tokens // blocks
    for b in range(blocks):
        s = pl.ds(b * rows, rows)
        a = a_all[layer, s]
        gate = dot(a, wg[0])
        up = dot(a, wu[0])
        ct = dot(dh[layer, s], wd[0], ((1,), (1,))).astype(BF).astype(F32)
        sig = jax.nn.sigmoid(gate)
        silu = gate * sig
        hid[s] = (silu * up).astype(BF)
        dup[s] = (ct * silu).astype(BF)
        dgate[s] = (ct * up * (sig + silu * (1.0 - sig))).astype(BF)

    @pl.when(layer == 1)
    def _():
        da[...] += dot(dgate[...], wg[0], ((1,), (1,))) + dot(dup[...], wu[0], ((1,), (1,)))

    at = at_all[layer]
    return dot(at, dgate[...]), dot(at, dup[...]), dot(hid[...], dh[layer], ((0,), (0,)))


def reduce_kernel(a_all, at_all, dy, h1, wg, wu, wd, out_g, out_u, out_d, *scratch):
    (hid, dgate, dup, da, dh,
     own_g, own_u, own_d, acc_g2, acc_u2, acc_g3, acc_u3, acc_d2, acc_d3,
     rg, ru, rd, sg, su, sd, sems) = scratch
    nx, ny, nz = GRID
    chunks = nx * ny
    total = 2 * chunks
    f = wg.shape[2]
    t = pl.program_id(0)
    at, neighbour = place()
    x_, y_, z_ = at

    senders = {
        name: Sender(axis, at, neighbour, *sem)
        for (name, axis), sem in zip(
            (("g1", 0), ("g2", 1), ("g3", 2), ("u1", 1), ("u2", 0), ("u3", 2), ("d1", 2), ("d2", 1), ("d3", 0)), sems, strict=True
        )
    }

    def halves(array, ref):
        if array in ("g1", "g2", "d1", "d2", "d3"):
            h = ref.shape[-2] // 2
            return ref.at[pl.ds(0, h)], ref.at[pl.ds(h, h)]
        if array == "u1":
            return ref.at[pl.ds(0, nx // 2)], ref.at[pl.ds(nx // 2, nx // 2)]
        if array == "u2":
            h = ref.shape[-2] // 2
            return ref.at[pl.ds(0, h)], ref.at[pl.ds(h, h)]
        h = ref.shape[-1] // 2
        return ref.at[:, pl.ds(0, h)], ref.at[:, pl.ds(h, h)]

    def first(array, slot, own, recv):
        s = senders[array]

        def start():
            for d, half in enumerate(halves(array, own(s.block(s.n // 2)))):
                s.copy(0, slot, d, half, recv[0].at[slot, d]).start()

        def middle(j):
            s.wait(j - 1, slot, [recv[j - 1].at[slot, d] for d in (0, 1)])
            q = s.n // 2 - j
            for d in (0, 1):
                block = own(s.block(q if d == 0 else -q))
                into = halves(array, block)[d] if j == 1 else block
                into[...] = (into[...].astype(F32) + recv[j - 1][slot, d].astype(F32)).astype(BF)
                s.copy(j, slot, d, block, recv[j].at[slot, d]).start()

        def last():
            j = s.n // 2
            s.wait(j - 1, slot, [recv[j - 1].at[slot, d] for d in (0, 1)])
            return own(s.p)[...].astype(F32) + recv[j - 1][slot, 0].astype(F32) + recv[j - 1][slot, 1].astype(F32)

        return start, middle, last

    def later(array, slot, own, recv, stage):
        s = senders[array]

        def start():
            for d, half in enumerate(halves(array, own(s.block(s.n // 2)))):
                stage[0][slot, d] = half[...].astype(BF)
                s.copy(0, slot, d, stage[0].at[slot, d], recv[0].at[slot, d]).start()

        def middle(j):
            s.wait(j - 1, slot, [recv[j - 1].at[slot, d] for d in (0, 1)])
            q = s.n // 2 - j
            for d in (0, 1):
                block = own(s.block(q if d == 0 else -q))
                into = halves(array, block)[d] if j == 1 else block
                into[...] = into[...] + recv[j - 1][slot, d].astype(F32)
                stage[j][slot, d] = block[...].astype(BF)
                s.copy(j, slot, d, stage[j].at[slot, d], recv[j].at[slot, d]).start()

        def last():
            j = s.n // 2
            s.wait(j - 1, slot, [recv[j - 1].at[slot, d] for d in (0, 1)])
            return own(s.p)[...] + recv[j - 1][slot, 0].astype(F32) + recv[j - 1][slot, 1].astype(F32)

        return start, middle, last

    def at_stage(k, every=1):
        def run(fn):
            c = t - LAG * k
            on = (c >= 0) & (c < total)
            if every > 1:
                on &= lax.rem(c, every) == every - 1
            pl.when(on)(functools.partial(fn, c))

        return run

    def columns(c):
        return pl.ds(pl.multiple_of(lax.rem(c, chunks) * f, f), f)

    def layer_of(c):
        return 1 - lax.div(c, chunks)

    @pl.when(t == 0)
    def _():
        meet(neighbour)
        dh[1] = dy[...]
        da[...] = jnp.zeros_like(da)

    def wide(which, own, acc2, acc3, recv, stage, out):
        def own1(slot):
            return (lambda q: own.at[slot, q]) if which == "g" else (lambda q: own.at[slot, :, q])

        def p1(c):
            slot = lax.rem(c, SLOTS)
            return first(which + "1", slot, own1(slot), recv[0:2])

        def p2(c):
            slot = lax.rem(c, SLOTS)
            return later(which + "2", slot, lambda q: acc2.at[slot, q], recv[2:4], stage[0:2])

        def p3(c):
            slot, long = lax.rem(c, SLOTS), lax.rem(c, 2 * SLOTS)
            return later(which + "3", slot, lambda q: acc3.at[long, q], recv[4:8], stage[2:6])

        def end(c):
            out[layer_of(c), :, columns(c)] = p3(c)[2]()

        at_stage(8)(end)
        for j in (3, 2, 1):
            at_stage(4 + j)(lambda c, j=j: p3(c)[1](j))

        def turn2(c):
            done = p2(c)[2]()
            rows = acc3.shape[2]
            for q in range(nz):
                acc3[lax.rem(c, 2 * SLOTS), q] = done[q * rows:(q + 1) * rows]
            p3(c)[0]()

        at_stage(4)(turn2)
        at_stage(3)(lambda c: p2(c)[1](1))

        def turn1(c):
            done = p1(c)[2]()
            acc2[lax.rem(c, SLOTS)] = done.reshape(acc2.shape[1:])
            p2(c)[0]()

        at_stage(2)(turn1)
        at_stage(1)(lambda c: p1(c)[1](1))

    wide("g", own_g, acc_g2, acc_g3, rg, sg, out_g)
    wide("u", own_u, acc_u2, acc_u3, ru, su, out_u)

    def d1(c):
        slot, long = lax.rem(c, SLOTS), lax.rem(c, 2 * SLOTS)
        return first("d1", slot, lambda q: own_d.at[long, q], rd[0:4])

    def d2(c):
        slot = lax.rem(lax.div(c, ny), 2)
        return later("d2", slot, lambda q: acc_d2.at[slot, q], rd[4:6], sd[0:2])

    def d3(c):
        slot = layer_of(c)
        return later("d3", slot, lambda q: acc_d3.at[slot, q], rd[6:8], sd[2:4])

    def d_end(c):
        out_d[layer_of(c)] = d3(c)[2]()

    at_stage(8, chunks)(d_end)
    at_stage(7, chunks)(lambda c: d3(c)[1](1))

    def d_turn2(c):
        acc_d3[layer_of(c), lax.rem(lax.div(c, ny), nx)] = d2(c)[2]()

    at_stage(6, ny)(d_turn2)
    at_stage(6, chunks)(lambda c: d3(c)[0]())
    at_stage(5, ny)(lambda c: d2(c)[1](1))

    def d_turn1(c):
        acc_d2[lax.rem(lax.div(c, ny), 2), lax.rem(c, ny)] = d1(c)[2]()

    at_stage(4)(d_turn1)
    at_stage(4, ny)(lambda c: d2(c)[0]())
    for j in (3, 2, 1):
        at_stage(j)(lambda c, j=j: d1(c)[1](j))

    @pl.when(t == chunks)
    def _():
        h, by_a = h1[...].astype(F32), da[...].astype(BF).astype(F32)
        scale = lax.rsqrt(jnp.mean(h**2, -1, keepdims=True) + 1e-6)
        by_h = scale * by_a - h * (scale**3 * jnp.mean(by_a * h, -1, keepdims=True))
        dh[0] = dy[...] + by_h.astype(BF)

    def produce(c):
        g, u, d = compute(layer_of(c), 4, a_all, at_all, dh, wg, wu, wd, hid, dgate, dup, da)
        slot, long = lax.rem(c, SLOTS), lax.rem(c, 2 * SLOTS)
        own_g[slot] = g.astype(BF).reshape(own_g.shape[1:])
        own_u[slot] = u.astype(BF).reshape(own_u.shape[1:])
        own_d[long] = d.astype(BF).reshape(own_d.shape[1:])
        p = lax.rem(c, SLOTS)
        first("g1", p, lambda q: own_g.at[slot, q], rg[0:2])[0]()
        first("u1", p, lambda q: own_u.at[slot, :, q], ru[0:2])[0]()
        first("d1", p, lambda q: own_d.at[long, q], rd[0:4])[0]()

    at_stage(0)(produce)


def gradients(x, dy, wg, wu, wd):
    nx, ny, nz = GRID
    n = nx * ny * nz
    tokens, d = x.shape
    ff = wg.shape[2]
    chunks = nx * ny
    f, rg, rd = ff // chunks, d // n, ff // n
    a_all, at_all, h1 = forward(x, wg, wu, wd)
    total = 2 * chunks

    def chunk(t):
        c = t - lax.div(t, total) * (t - total + 1)
        return 1 - lax.div(c, chunks), lax.rem(c, chunks)

    def cols(t):
        layer, c = chunk(t)
        return layer, 0, c

    def rows(t):
        layer, c = chunk(t)
        return layer, c, 0

    def wide_recv(outer, inner):
        a, b = outer
        r1 = [(a // 2, b), (a, b)]
        return r1

    s, long = SLOTS, 2 * SLOTS
    g_blocks = [((ny * nz * rg) // 2, f), (ny * nz * rg, f), (nz * rg // 2, f), (nz * rg, f), (rg, f // 2), (rg, f), (rg, f), (rg, f)]
    u_blocks = [(nx // 2, nz * rg, f), (nx, nz * rg, f), (nz * rg // 2, f), (nz * rg, f), (rg, f // 2), (rg, f), (rg, f), (rg, f)]
    if nz == 4:
        g_blocks, u_blocks = g_blocks[:6], u_blocks[:6]
    d_blocks = [(rd // 2, d)] + [(rd, d)] * (nz // 2 - 1) + [(rd // 2, d), (rd, d)] * 2
    d_slots = [s] * (nz // 2) + [2] * 4
    steps = {"g1": nx, "g2": ny, "g3": nz, "u1": ny, "u2": nx, "u3": nz, "d1": nz, "d2": ny, "d3": nx}
    dma = pltpu.SemaphoreType.DMA

    def sems(name, n):
        count = 2 if name in ("d2", "d3") else s
        return (dma((n // 2, count, 2)), dma((n // 2, count, 2)))

    scratch = [
        pltpu.VMEM((tokens, f), BF), pltpu.VMEM((tokens, f), BF), pltpu.VMEM((tokens, f), BF),
        pltpu.VMEM((tokens, d), F32), pltpu.VMEM((2, tokens, d), BF),
        pltpu.VMEM((s, nx, ny * nz * rg, f), BF), pltpu.VMEM((s, nx, ny, nz * rg, f), BF), pltpu.VMEM((long, nz, rd, d), BF),
        pltpu.VMEM((s, ny, nz * rg, f), F32), pltpu.VMEM((s, nx, nz * rg, f), F32),
        pltpu.VMEM((long, nz, rg, f), F32), pltpu.VMEM((long, nz, rg, f), F32),
        pltpu.VMEM((2, ny, rd, d), F32), pltpu.VMEM((2, nx, rd, d), F32),
        [pltpu.VMEM((s, 2, *b), BF) for b in g_blocks],
        [pltpu.VMEM((s, 2, *b), BF) for b in u_blocks],
        [pltpu.VMEM((k, 2, *b), BF) for k, b in zip(d_slots, d_blocks, strict=True)],
        [pltpu.VMEM((s, 2, *b), BF) for b in g_blocks[2:]],
        [pltpu.VMEM((s, 2, *b), BF) for b in u_blocks[2:]],
        [pltpu.VMEM((k, 2, *b), BF) for k, b in zip(d_slots[nz // 2:], d_blocks[nz // 2:], strict=True)],
        [sems(name, n) for name, n in steps.items()],
    ]
    vmem = pl.BlockSpec(memory_space=pltpu.VMEM)
    return pl.pallas_call(
        reduce_kernel,
        grid=(total + 8 * LAG,),
        in_specs=[vmem] * 4 + [pl.BlockSpec((1, d, f), cols), pl.BlockSpec((1, d, f), cols), pl.BlockSpec((1, f, d), rows)],
        out_specs=[vmem] * 3,
        out_shape=[jax.ShapeDtypeStruct((2, rg, ff), F32)] * 2 + [jax.ShapeDtypeStruct((2, rd, d), F32)],
        scratch_shapes=scratch,
        compiler_params=pltpu.CompilerParams(
            vmem_limit_bytes=VMEM_LIMIT, collective_id=0, has_side_effects=True, dimension_semantics=("arbitrary",)
        ),
        name="reduce",
    )(a_all, at_all, dy, h1, wg, wu, wd)


def gather_kernel(jobs, ng, nu, nd, og, ou, od, *scratch):
    zg, zu, yg, yu, local, sems = scratch
    nx, ny, nz = GRID
    total = 2 * jobs
    f = zg.shape[-1]
    r = nd.shape[1] // jobs
    at, neighbour = place()
    x_, y_, z_ = at
    meet(neighbour)
    names = (("g1", 2), ("g2", 1), ("g3", 0), ("u1", 2), ("u2", 0), ("u3", 1), ("d1", 0), ("d2", 1), ("d3", 2))
    senders = {name: Sender(axis, at, neighbour, *sem) for (name, axis), sem in zip(names, sems, strict=True)}

    def piece(j):
        return 1 - lax.div(j, jobs), lax.rem(j, jobs)

    def blocks(name, j, slot):
        layer, q = piece(j)
        cols = pl.ds(pl.multiple_of(q * f, f), f)
        rows = pl.ds(pl.multiple_of(q * r, r), r)
        zs = lax.rem(j, 2 * SLOTS)
        h = nz * ng.shape[1] // 2
        return {
            "g1": (lambda b: zg.at[zs, b], lambda b: (zg.at[zs, b, :, pl.ds(0, f // 2)], zg.at[zs, b, :, pl.ds(f // 2, f // 2)])),
            "u1": (lambda b: zu.at[zs, b], lambda b: (zu.at[zs, b, :, pl.ds(0, f // 2)], zu.at[zs, b, :, pl.ds(f // 2, f // 2)])),
            "g2": (lambda b: og.at[layer, x_, b, :, cols], lambda b: (og.at[layer, x_, b, pl.ds(0, h), cols], og.at[layer, x_, b, pl.ds(h, h), cols])),
            "u2": (lambda b: ou.at[layer, b, y_, :, cols], lambda b: (ou.at[layer, b, y_, pl.ds(0, h), cols], ou.at[layer, b, y_, pl.ds(h, h), cols])),
            "g3": (lambda b: og.at[layer, b, :, :, cols], lambda b: (og.at[layer, b, pl.ds(0, ny // 2), :, cols], og.at[layer, b, pl.ds(ny // 2, ny // 2), :, cols])),
            "u3": (lambda b: ou.at[layer, :, b, :, cols], lambda b: (ou.at[layer, pl.ds(0, nx // 2), b, :, cols], ou.at[layer, pl.ds(nx // 2, nx // 2), b, :, cols])),
            "d1": (lambda b: od.at[layer, b, y_, z_, rows], lambda b: (od.at[layer, b, y_, z_, pl.ds(q * r, r // 2)], od.at[layer, b, y_, z_, pl.ds(q * r + r // 2, r // 2)])),
            "d2": (lambda b: od.at[layer, :, b, z_, rows], lambda b: (od.at[layer, pl.ds(0, nx // 2), b, z_, rows], od.at[layer, pl.ds(nx // 2, nx // 2), b, z_, rows])),
            "d3": (lambda b: od.at[layer, :, :, b, rows], lambda b: (od.at[layer, pl.ds(0, nx // 2), :, b, rows], od.at[layer, pl.ds(nx // 2, nx // 2), :, b, rows])),
        }[name]

    def ring(name, j, i, first=None):
        slot = lax.rem(j, SLOTS)
        s = senders[name]
        full, half = blocks(name, j, slot)
        if i > 0:
            arrived(name, j, i - 1)
        for d in (0, 1):
            b = s.block(-i if d == 0 else i)
            dst = full(b) if i < s.n // 2 - 1 else half(b)[d]
            s.copy(i, slot, d, first if first is not None else dst, dst).start()

    def arrived(name, j, i):
        slot = lax.rem(j, SLOTS)
        s = senders[name]
        full, half = blocks(name, j, slot)
        refs = []
        for d in (0, 1):
            b = s.block(-1 - i if d == 0 else 1 + i)
            refs.append(full(b) if i < s.n // 2 - 1 else half(b)[d])
        s.wait(i, slot, refs)

    def tick(t, carry):
        def at_stage(k, fn):
            j = t - LAG * k
            pl.when((j >= 0) & (j < total))(lambda: fn(j))

        def wide(which, new, zb, yb, which_local):
            p1, p2, p3 = (which + k for k in "123")

            def keep(j):
                slot = lax.rem(j, SLOTS)
                own = blocks(p2, j, slot)[0](y_ if which == "g" else x_)
                return pltpu.make_async_copy(yb.at[slot], own, local.at[which_local, slot])

            def begin(j):
                layer, q = piece(j)
                zb[lax.rem(j, 2 * SLOTS), z_] = new[layer, :, pl.ds(pl.multiple_of(q * f, f), f)]
                ring(p1, j, 0)

            def turn(j):
                slot = lax.rem(j, SLOTS)
                arrived(p1, j, nz // 2 - 1)
                yb[slot] = zb[lax.rem(j, 2 * SLOTS)].reshape(yb.shape[1:])
                keep(j).start()
                ring(p2, j, 0, yb.at[slot])

            def turn2(j):
                arrived(p2, j, 1)
                keep(j).wait()
                ring(p3, j, 0)

            k = nz // 2
            at_stage(k + 4, lambda j: arrived(p3, j, 1))
            at_stage(k + 3, lambda j: ring(p3, j, 1))
            at_stage(k + 2, turn2)
            at_stage(k + 1, lambda j: ring(p2, j, 1))
            at_stage(k, turn)
            for i in range(k - 1, 0, -1):
                at_stage(i, lambda j, i=i: ring(p1, j, i))
            at_stage(0, begin)

        wide("g", ng, zg, yg, 0)
        wide("u", nu, zu, yu, 1)

        def keep(j):
            slot = lax.rem(j, SLOTS)
            layer, q = piece(j)
            own = nd.at[layer, pl.ds(pl.multiple_of(q * r, r), r)]
            return own, pltpu.make_async_copy(own, blocks("d1", j, slot)[0](x_), local.at[2, slot])

        def d_begin(j):
            own, copy = keep(j)
            copy.start()
            ring("d1", j, 0, own)

        def d_turn(j):
            arrived("d1", j, 1)
            keep(j)[1].wait()
            ring("d2", j, 0)

        def d_turn2(j):
            arrived("d2", j, 1)
            ring("d3", j, 0)

        k = nz // 2
        at_stage(4 + k, lambda j: arrived("d3", j, k - 1))
        for i in range(k - 1, 0, -1):
            at_stage(4 + i, lambda j, i=i: ring("d3", j, i))
        at_stage(4, d_turn2)
        at_stage(3, lambda j: ring("d2", j, 1))
        at_stage(2, d_turn)
        at_stage(1, lambda j: ring("d1", j, 1))
        at_stage(0, d_begin)
        return carry

    lax.fori_loop(0, total + LAG * (nz // 2 + 4), tick, 0)


def gather(ng, nu, nd):
    nx, ny, nz = GRID
    _, rg, ff = ng.shape
    _, rd, d = nd.shape
    f = ff // JOBS
    dma = pltpu.SemaphoreType.DMA
    steps = (nz, ny, nx, nz, nx, ny, nx, ny, nz)
    wide = jax.ShapeDtypeStruct((2, nx, ny, nz * rg, ff), BF)
    og, ou, od = pl.pallas_call(
        functools.partial(gather_kernel, JOBS),
        in_specs=[pl.BlockSpec(memory_space=pltpu.VMEM)] * 3,
        out_specs=[pl.BlockSpec(memory_space=pl.ANY)] * 3,
        out_shape=[wide, wide, jax.ShapeDtypeStruct((2, nx, ny, nz, rd, d), BF)],
        scratch_shapes=[
            pltpu.VMEM((2 * SLOTS, nz, rg, f), BF), pltpu.VMEM((2 * SLOTS, nz, rg, f), BF),
            pltpu.VMEM((SLOTS, nz * rg, f), BF), pltpu.VMEM((SLOTS, nz * rg, f), BF),
            dma((3, SLOTS)),
            [(dma((n // 2, SLOTS, 2)), dma((n // 2, SLOTS, 2))) for n in steps],
        ],
        compiler_params=pltpu.CompilerParams(vmem_limit_bytes=VMEM_LIMIT, collective_id=1, has_side_effects=True),
        name="gather",
    )(ng, nu, nd)
    n = nx * ny * nz
    return og.reshape(2, n * rg, ff), ou.reshape(2, n * rg, ff), od.reshape(2, n * rd, d)


def adamw(w, m, v, g):
    g = lax.reduce_precision(g, 8, 7)
    m = 0.9 * m + 0.1 * g
    v = 0.95 * v + 0.05 * g * g
    step = m * lax.rsqrt(v + 1e-8) + 0.1 * w
    return (w - 0.02 * step).astype(BF), m, v


def device_step(x, dy, *arrays):
    weights, ms, vs = (arrays[i:i + 3] for i in (0, 3, 6))
    sums = gradients(x[0], dy[0], *weights)
    me = lax.axis_index("dp")
    new = []
    for w, m, v, g in zip(weights, ms, vs, sums, strict=True):
        rows = m.shape[1]
        own = lax.dynamic_slice_in_dim(w, me * rows, rows, 1).astype(F32)
        new.append(adamw(own, m, v, g))
    gathered = gather(*(one[0] for one in new))
    return (*gathered, *(one[1] for one in new), *(one[2] for one in new))


def solution(mesh):
    x, w, m = P(("rep", "dp"), None, None), P(None, None, None), P(None, "dp", None)
    return jax.shard_map(
        device_step,
        mesh=mesh,
        in_specs=(x, x, w, w, w, *[m] * 6),
        out_specs=(*[P("rep", None, None)] * 3, *[P("rep", "dp", None)] * 6),
        check_vma=False,
    )
```

time: 2910 us -> 516 us (0.18)
  blocking collectives: 1970 us -> 0 us
  Pallas kernels: 0 us -> 476 us
  waiting for transfers between devices: 470 us -> 0 us
  matrix products: 310 us -> 0 us
  other arithmetic: 72.1 us -> 5 us
    unnamed x1 -> x0, blocking collectives: 1970 us -> none
    pallas_call x0 -> x3, Pallas kernels: none -> 476 us  [the longest x1 245 us: gradients(): pl.pallas_call(reduce_kernel, grid=(total + 8 * LAG,), in_specs=[vmem] *...]
    reshape x3 -> x0, waiting for transfers between devices: 470 us -> none  [step(): t.reshape(-1, *t.shape[2:])]
    dot_general x15 -> x0, matrix products: 310 us -> none  [the longest x5 112 us: layer(): up = jnp.dot(a, w['w_up'], preferred_element_type=jnp.float32)]
    unnamed x3 -> x1, other arithmetic: 62.7 us -> 0.01 us
  transfers between devices with their start and end apart: 5 -> 0, of which waited for: 3 -> 0; matrix products, arithmetic and copies ran while one was open for 7% -> 0% of each run, Pallas kernels for 0% -> 0%
where the time goes in v1:
time: 516 us
  Pallas kernels  476 us (92%)
  local copies, waits for them, and re-layouts  34 us (7%)
    pallas_call x1, Pallas kernels, gradients(): pl.pallas_call(reduce_kernel, grid=(total + 8 * LAG,), in_specs=[vmem] *...  245 us
    pallas_call x1, Pallas kernels, gather(): pl.pallas_call(functools.partial(gather_kernel, JOBS), in_specs=[pl.Block...  197 us
    pallas_call x1, Pallas kernels, forward(): pl.pallas_call(forward_kernel, grid=(16,), in_specs=[pl.BlockSpec(memory_...  35 us
    unnamed x19, local copies, waits for them, and re-layouts  34 us

profile of v1, /device:TPU:2, one launch (start us, length us, event | category | flops | bytes accessed | tf_op | source)
XLA Modules:
  0.0 516.0 jit_solution(12960900963920705966)
XLA Ops:
  0.6 35.0 %forward.1 = (bf16[2,1024,512]{2,1,0:T(8,128)(2,1)}, bf16[2,512,1024]{2,1,0:T(8,128)(2,1)}, bf16[1024,512]{1,0:T(8,128)(2,1)}) custom-call(bf16[1024,512]{1,0:T(8,128)(2,1)} %bitcast.11, bf16[2,512,8192]{2,1,0:T(8,128)(2,1)} %wg.3, bf16[2,512,8192]{2,1,0:T(8,128)(2,1)} %wu.3, bf16[2,8192,512]{2,1,0:T(8,128)(2,1)} %wd.3), custom_call_target="tpu_custom_call" | custom-call | tf_op jit(solution)/shard_map/forward/pallas_call | solution.py:100
  35.7 0.0 copy-start.1
  35.7 0.0 copy-start.2
  35.7 0.0 copy-start.3
  35.7 244.7 %reduce.1 = (f32[2,4,8192]{2,1,0:T(4,128)}, f32[2,4,8192]{2,1,0:T(4,128)}, f32[2,64,512]{2,1,0:T(8,128)}) custom-call(bf16[2,1024,512]{2,1,0:T(8,128)(2,1)} %get-tuple-element.18.a_all, bf16[2,512,1024]{2,1,0:T(8,128)(2,1)} %get-tuple-element.19.at_all, bf16[1024,512]{1,0:T(8,128)(2,1)} %bitcast.10, bf16[1024,512]{1,0:T(8,128)(2,1)} %get-tuple-element.20.h1, ...), custom_call_target="tpu_custom_call" | custom-call | tf_op jit(solution)/shard_map/reduce/pallas_call | solution.py:400
  280.3 0.0 copy-done.1
  280.3 0.0 copy-done.2
  280.4 1.9 fusion.8
  282.3 0.0 copy-done.3
  282.3 3.1 fusion.2
  285.4 196.5 %gather.1 = (bf16[2,4,4,32,8192]{4,3,2,1,0:T(8,128)(2,1)}, bf16[2,4,4,32,8192]{4,3,2,1,0:T(8,128)(2,1)}, bf16[2,4,4,8,64,512]{5,4,3,2,1,0:T(8,128)(2,1)}) custom-call(bf16[2,4,8192]{2,1,0:T(4,128)(2,1)} %get-tuple-element.33.ng, bf16[2,4,8192]{2,1,0:T(4,128)(2,1)} %get-tuple-element.36.nu, bf16[2,64,512]{2,1,0:T(8,128)(2,1)} %get-tuple-element.27.nd), custom_call_target="tpu_custom_call" | custom-call | tf_op jit(solution)/shard_map/gather/pallas_call | solution.py:553
  481.9 0.0 copy-start
  481.9 0.0 slice-start
  481.9 0.0 slice-start.1
  481.9 16.7 %copy.23 = bf16[2,512,8192]{2,1,0:T(8,128)(2,1)} copy(bf16[2,512,8192]{2,1,0:T(8,128)(2,1)} %bitcast.9) | data formatting | bytes 33554432
  498.6 0.0 copy-done
  498.6 0.0 slice-start.2
  498.6 0.0 slice-start.3
  498.6 8.5 %copy.24 = bf16[2,512,8192]{2,1,0:T(8,128)(2,1)} copy(bf16[2,512,8192]{2,1,0:T(8,128)(2,1)S(1)} %bitcast.8) | data formatting | bytes 33554432
  507.1 0.0 slice-done
  507.1 0.0 slice-done.1
  507.1 1.5 slice-done.2
  508.6 1.2 slice-done.3
  509.8 6.2 %copy.25 = bf16[2,8192,512]{2,1,0:T(8,128)(2,1)} copy(bf16[2,8192,512]{2,1,0:T(8,128)(2,1)S(1)} %bitcast.7) | data formatting | bytes 33554432
  (1 shorter events, 0.0 us)
Async XLA Ops:
  35.7 244.7 %copy-start.1 = (f32[2,64,512]{2,1,0:T(8,128)S(1)}, f32[2,64,512]{2,1,0:T(8,128)}, u32[]{:S(2)}) copy-start(f32[2,64,512]{2,1,0:T(8,128)} %param.21) | copy-start | bytes 786436
  35.7 244.7 %copy-start.2 = (f32[2,64,512]{2,1,0:T(8,128)S(1)}, f32[2,64,512]{2,1,0:T(8,128)}, u32[]{:S(2)}) copy-start(f32[2,64,512]{2,1,0:T(8,128)} %param.18) | copy-start | bytes 786436
  35.7 246.6 %copy-start.3 = (f32[2,4,8192]{2,1,0:T(4,128)S(1)}, f32[2,4,8192]{2,1,0:T(4,128)}, u32[]{:S(2)}) copy-start(f32[2,4,8192]{2,1,0:T(4,128)} %param.19) | copy-start | bytes 786436
  481.9 16.7 %copy-start = (bf16[2,4,4,32,8192]{4,3,2,1,0:T(8,128)(2,1)S(1)}, bf16[2,4,4,32,8192]{4,3,2,1,0:T(8,128)(2,1)}, u32[]{:S(2)}) copy-start(bf16[2,4,4,32,8192]{4,3,2,1,0:T(8,128)(2,1)} %get-tuple-element.25) | copy-start | bytes 50331652
  481.9 25.2 %slice-start = ((s8[16777216]{0:T(1024)(128)(4,1)}), s8[4194304]{0:T(1024)(128)(4,1)S(1)}, s32[]{:S(2)}) async-start(s8[16777216]{0:T(1024)(128)(4,1)} %bitcast.5), calls=%async_computation | async-start | bytes 8388608
  481.9 25.2 %slice-start.1 = ((s8[16777216]{0:T(1024)(128)(4,1)}), s8[4194304]{0:T(1024)(128)(4,1)S(1)}, s32[]{:S(2)}) async-start(s8[16777216]{0:T(1024)(128)(4,1)} %bitcast.5), calls=%async_computation.1 | async-start | bytes 8388608
  498.6 10.0 %slice-start.2 = ((s8[16777216]{0:T(1024)(128)(4,1)}), s8[4194304]{0:T(1024)(128)(4,1)S(1)}, s32[]{:S(2)}) async-start(s8[16777216]{0:T(1024)(128)(4,1)} %bitcast.5), calls=%async_computation.2 | async-start | bytes 8388608
  498.6 11.2 %slice-start.3 = ((s8[16777216]{0:T(1024)(128)(4,1)}), s8[4194304]{0:T(1024)(128)(4,1)S(1)}, s32[]{:S(2)}) async-start(s8[16777216]{0:T(1024)(128)(4,1)} %bitcast.5), calls=%async_computation.3 | async-start | bytes 8388608

commit v2 on v1

--- a/solution.py
+++ b/solution.py
@@ -11,9 +11,10 @@
 BF, F32 = jnp.bfloat16, jnp.float32
 MESH = pl.DeviceIdType.MESH
 VMEM_LIMIT = 66_000_000
+GATHER_VMEM = 12 << 20
 LAG = 2
 SLOTS = 6
-JOBS = 4
+JOBS = 8
 
 
 def dot(a, b, dims=((1,), (0,))):
@@ -67,55 +68,6 @@
             c = self.copy(step, slot, d, refs[d], refs[d])
             c.wait_recv()
             c.wait_send()
-
-
-def forward_kernel(x_ref, wg, wu, wd, a_all, at_all, h1, acc):
-    i = pl.program_id(0)
-
-    @pl.when(i == 0)
-    def _():
-        a = normed(x_ref[...])
-        a_all[0] = a
-        at_all[0] = a.T
-        acc[...] = jnp.zeros_like(acc)
-
-    a = a_all[0]
-    gate = dot(a, wg[0])
-    up = dot(a, wu[0])
-    hidden = (gate * jax.nn.sigmoid(gate) * up).astype(BF)
-    acc[...] += dot(hidden, wd[0])
-
-    @pl.when(i == pl.num_programs(0) - 1)
-    def _():
-        h = x_ref[...] + acc[...].astype(BF)
-        h1[...] = h
-        a = normed(h)
-        a_all[1] = a
-        at_all[1] = a.T
-
-
-def forward(x, wg, wu, wd):
-    (tokens, d), ff = x.shape, wg.shape[2]
-    f = ff // 16
-    return pl.pallas_call(
-        forward_kernel,
-        grid=(16,),
-        in_specs=[
-            pl.BlockSpec(memory_space=pltpu.VMEM),
-            pl.BlockSpec((1, d, f), lambda i: (0, 0, i)),
-            pl.BlockSpec((1, d, f), lambda i: (0, 0, i)),
-            pl.BlockSpec((1, f, d), lambda i: (0, i, 0)),
-        ],
-        out_specs=[pl.BlockSpec(memory_space=pltpu.VMEM)] * 3,
-        out_shape=[
-            jax.ShapeDtypeStruct((2, tokens, d), BF),
-            jax.ShapeDtypeStruct((2, d, tokens), BF),
-            jax.ShapeDtypeStruct((tokens, d), BF),
-        ],
-        scratch_shapes=[pltpu.VMEM((tokens, d), F32)],
-        compiler_params=pltpu.CompilerParams(vmem_limit_bytes=VMEM_LIMIT, dimension_semantics=("arbitrary",)),
-        name="forward",
-    )(x, wg, wu, wd)
 
 
 def compute(layer, blocks, a_all, at_all, dh, wg, wu, wd, hid, dgate, dup, da):
@@ -133,23 +85,30 @@
         dup[s] = (ct * silu).astype(BF)
         dgate[s] = (ct * up * (sig + silu * (1.0 - sig))).astype(BF)
 
-    @pl.when(layer == 1)
-    def _():
+    if layer == 1:
         da[...] += dot(dgate[...], wg[0], ((1,), (1,))) + dot(dup[...], wu[0], ((1,), (1,)))
 
     at = at_all[layer]
     return dot(at, dgate[...]), dot(at, dup[...]), dot(hid[...], dh[layer], ((0,), (0,)))
 
 
-def reduce_kernel(a_all, at_all, dy, h1, wg, wu, wd, out_g, out_u, out_d, *scratch):
-    (hid, dgate, dup, da, dh,
+def once(on, fn):
+    def body(_, carry):
+        fn()
+        return carry
+
+    lax.fori_loop(0, on.astype(jnp.int32), body, 0)
+
+
+def reduce_kernel(x, dy, wg, wu, wd, out_g, out_u, out_d, *scratch):
+    (hid, dgate, dup, da, dh, a_all, at_all, h1,
      own_g, own_u, own_d, acc_g2, acc_u2, acc_g3, acc_u3, acc_d2, acc_d3,
      rg, ru, rd, sg, su, sd, sems) = scratch
     nx, ny, nz = GRID
     chunks = nx * ny
     total = 2 * chunks
     f = wg.shape[2]
-    t = pl.program_id(0)
+    t = pl.program_id(0) - chunks
     at, neighbour = place()
     x_, y_, z_ = at
 
@@ -236,11 +195,34 @@
     def layer_of(c):
         return 1 - lax.div(c, chunks)
 
-    @pl.when(t == 0)
-    def _():
+    def enter(layer, h):
+        a = normed(h)
+        a_all[layer] = a
+        at_all[layer] = a.T
+
+    def begin():
         meet(neighbour)
+        enter(0, x[...])
         dh[1] = dy[...]
         da[...] = jnp.zeros_like(da)
+
+    def between():
+        h = x[...] + da[...].astype(BF)
+        h1[...] = h
+        enter(1, h)
+        da[...] = jnp.zeros_like(da)
+
+    once(t == -chunks, begin)
+    once(t == 0, between)
+
+    @pl.when(t < 0)
+    def _():
+        rows = hid.shape[0] // 2
+        for b in range(2):
+            s = pl.ds(b * rows, rows)
+            gate = dot(a_all[0, s], wg[0])
+            up = dot(a_all[0, s], wu[0])
+            da[s] += dot((gate * jax.nn.sigmoid(gate) * up).astype(BF), wd[0])
 
     def wide(which, own, acc2, acc3, recv, stage, out):
         def own1(slot):
@@ -319,15 +301,16 @@
     for j in (3, 2, 1):
         at_stage(j)(lambda c, j=j: d1(c)[1](j))
 
-    @pl.when(t == chunks)
-    def _():
+    def backward_norm():
         h, by_a = h1[...].astype(F32), da[...].astype(BF).astype(F32)
         scale = lax.rsqrt(jnp.mean(h**2, -1, keepdims=True) + 1e-6)
         by_h = scale * by_a - h * (scale**3 * jnp.mean(by_a * h, -1, keepdims=True))
         dh[0] = dy[...] + by_h.astype(BF)
 
-    def produce(c):
-        g, u, d = compute(layer_of(c), 4, a_all, at_all, dh, wg, wu, wd, hid, dgate, dup, da)
+    once(t == chunks, backward_norm)
+
+    def produce(c, layer):
+        g, u, d = compute(layer, 4, a_all, at_all, dh, wg, wu, wd, hid, dgate, dup, da)
         slot, long = lax.rem(c, SLOTS), lax.rem(c, 2 * SLOTS)
         own_g[slot] = g.astype(BF).reshape(own_g.shape[1:])
         own_u[slot] = u.astype(BF).reshape(own_u.shape[1:])
@@ -337,7 +320,8 @@
         first("u1", p, lambda q: own_u.at[slot, :, q], ru[0:2])[0]()
         first("d1", p, lambda q: own_d.at[long, q], rd[0:4])[0]()
 
-    at_stage(0)(produce)
+    for layer in (1, 0):
+        pl.when((t >= (1 - layer) * chunks) & (t < (2 - layer) * chunks))(functools.partial(produce, t, layer))
 
 
 def gradients(x, dy, wg, wu, wd):
@@ -347,12 +331,11 @@
     ff = wg.shape[2]
     chunks = nx * ny
     f, rg, rd = ff // chunks, d // n, ff // n
-    a_all, at_all, h1 = forward(x, wg, wu, wd)
     total = 2 * chunks
 
     def chunk(t):
-        c = t - lax.div(t, total) * (t - total + 1)
-        return 1 - lax.div(c, chunks), lax.rem(c, chunks)
+        c = t - lax.div(t, 3 * chunks) * (t - 3 * chunks + 1)
+        return lax.rem(lax.div(c, chunks), 2), lax.rem(c, chunks)
 
     def cols(t):
         layer, c = chunk(t)
@@ -361,11 +344,6 @@
     def rows(t):
         layer, c = chunk(t)
         return layer, c, 0
-
-    def wide_recv(outer, inner):
-        a, b = outer
-        r1 = [(a // 2, b), (a, b)]
-        return r1
 
     s, long = SLOTS, 2 * SLOTS
     g_blocks = [((ny * nz * rg) // 2, f), (ny * nz * rg, f), (nz * rg // 2, f), (nz * rg, f), (rg, f // 2), (rg, f), (rg, f), (rg, f)]
@@ -384,6 +362,7 @@
     scratch = [
         pltpu.VMEM((tokens, f), BF), pltpu.VMEM((tokens, f), BF), pltpu.VMEM((tokens, f), BF),
         pltpu.VMEM((tokens, d), F32), pltpu.VMEM((2, tokens, d), BF),
+        pltpu.VMEM((2, tokens, d), BF), pltpu.VMEM((2, d, tokens), BF), pltpu.VMEM((tokens, d), BF),
         pltpu.VMEM((s, nx, ny * nz * rg, f), BF), pltpu.VMEM((s, nx, ny, nz * rg, f), BF), pltpu.VMEM((long, nz, rd, d), BF),
         pltpu.VMEM((s, ny, nz * rg, f), F32), pltpu.VMEM((s, nx, nz * rg, f), F32),
         pltpu.VMEM((long, nz, rg, f), F32), pltpu.VMEM((long, nz, rg, f), F32),
@@ -399,8 +378,8 @@
     vmem = pl.BlockSpec(memory_space=pltpu.VMEM)
     return pl.pallas_call(
         reduce_kernel,
-        grid=(total + 8 * LAG,),
-        in_specs=[vmem] * 4 + [pl.BlockSpec((1, d, f), cols), pl.BlockSpec((1, d, f), cols), pl.BlockSpec((1, f, d), rows)],
+        grid=(chunks + total + 8 * LAG,),
+        in_specs=[vmem] * 2 + [pl.BlockSpec((1, d, f), cols), pl.BlockSpec((1, d, f), cols), pl.BlockSpec((1, f, d), rows)],
         out_specs=[vmem] * 3,
         out_shape=[jax.ShapeDtypeStruct((2, rg, ff), F32)] * 2 + [jax.ShapeDtypeStruct((2, rd, d), F32)],
         scratch_shapes=scratch,
@@ -408,7 +387,7 @@
             vmem_limit_bytes=VMEM_LIMIT, collective_id=0, has_side_effects=True, dimension_semantics=("arbitrary",)
         ),
         name="reduce",
-    )(a_all, at_all, dy, h1, wg, wu, wd)
+    )(x, dy, wg, wu, wd)
 
 
 def gather_kernel(jobs, ng, nu, nd, og, ou, od, *scratch):
@@ -422,6 +401,7 @@
     meet(neighbour)
     names = (("g1", 2), ("g2", 1), ("g3", 0), ("u1", 2), ("u2", 0), ("u3", 1), ("d1", 0), ("d2", 1), ("d3", 2))
     senders = {name: Sender(axis, at, neighbour, *sem) for (name, axis), sem in zip(names, sems, strict=True)}
+    senders |= {"e1": Sender(1, at, neighbour, *sems[6]), "e2": Sender(0, at, neighbour, *sems[7])}
 
     def piece(j):
         return 1 - lax.div(j, jobs), lax.rem(j, jobs)
@@ -431,6 +411,7 @@
         cols = pl.ds(pl.multiple_of(q * f, f), f)
         rows = pl.ds(pl.multiple_of(q * r, r), r)
         zs = lax.rem(j, 2 * SLOTS)
+        left, right = pl.ds(0, nd.shape[2] // 2), pl.ds(nd.shape[2] // 2, nd.shape[2] // 2)
         h = nz * ng.shape[1] // 2
         return {
             "g1": (lambda b: zg.at[zs, b], lambda b: (zg.at[zs, b, :, pl.ds(0, f // 2)], zg.at[zs, b, :, pl.ds(f // 2, f // 2)])),
@@ -439,8 +420,10 @@
             "u2": (lambda b: ou.at[layer, b, y_, :, cols], lambda b: (ou.at[layer, b, y_, pl.ds(0, h), cols], ou.at[layer, b, y_, pl.ds(h, h), cols])),
             "g3": (lambda b: og.at[layer, b, :, :, cols], lambda b: (og.at[layer, b, pl.ds(0, ny // 2), :, cols], og.at[layer, b, pl.ds(ny // 2, ny // 2), :, cols])),
             "u3": (lambda b: ou.at[layer, :, b, :, cols], lambda b: (ou.at[layer, pl.ds(0, nx // 2), b, :, cols], ou.at[layer, pl.ds(nx // 2, nx // 2), b, :, cols])),
-            "d1": (lambda b: od.at[layer, b, y_, z_, rows], lambda b: (od.at[layer, b, y_, z_, pl.ds(q * r, r // 2)], od.at[layer, b, y_, z_, pl.ds(q * r + r // 2, r // 2)])),
+            "d1": (lambda b: od.at[layer, b, y_, z_, rows], lambda b: (od.at[layer, b, y_, z_, rows, left], od.at[layer, b, y_, z_, rows, right])),
+            "e1": (lambda b: od.at[layer, x_, b, z_, rows], lambda b: (od.at[layer, x_, b, z_, rows, left], od.at[layer, x_, b, z_, rows, right])),
             "d2": (lambda b: od.at[layer, :, b, z_, rows], lambda b: (od.at[layer, pl.ds(0, nx // 2), b, z_, rows], od.at[layer, pl.ds(nx // 2, nx // 2), b, z_, rows])),
+            "e2": (lambda b: od.at[layer, b, :, z_, rows], lambda b: (od.at[layer, b, pl.ds(0, ny // 2), z_, rows], od.at[layer, b, pl.ds(ny // 2, ny // 2), z_, rows])),
             "d3": (lambda b: od.at[layer, :, :, b, rows], lambda b: (od.at[layer, pl.ds(0, nx // 2), :, b, rows], od.at[layer, pl.ds(nx // 2, nx // 2), :, b, rows])),
         }[name]
 
@@ -514,29 +497,33 @@
             own = nd.at[layer, pl.ds(pl.multiple_of(q * r, r), r)]
             return own, pltpu.make_async_copy(own, blocks("d1", j, slot)[0](x_), local.at[2, slot])
 
-        def d_begin(j):
+        def d_begin(name, j):
             own, copy = keep(j)
             copy.start()
-            ring("d1", j, 0, own)
-
-        def d_turn(j):
-            arrived("d1", j, 1)
+            ring(name + "1", j, 0, own)
+
+        def d_turn(name, j):
+            arrived(name + "1", j, 1)
             keep(j)[1].wait()
-            ring("d2", j, 0)
-
-        def d_turn2(j):
-            arrived("d2", j, 1)
+            ring(name + "2", j, 0)
+
+        def d_turn2(name, j):
+            arrived(name + "2", j, 1)
             ring("d3", j, 0)
+
+        def either(k, fn):
+            at_stage(k, lambda j: pl.when(lax.rem(j, 2) == 0)(lambda: fn("d", j)))
+            at_stage(k, lambda j: pl.when(lax.rem(j, 2) == 1)(lambda: fn("e", j)))
 
         k = nz // 2
         at_stage(4 + k, lambda j: arrived("d3", j, k - 1))
         for i in range(k - 1, 0, -1):
             at_stage(4 + i, lambda j, i=i: ring("d3", j, i))
-        at_stage(4, d_turn2)
-        at_stage(3, lambda j: ring("d2", j, 1))
-        at_stage(2, d_turn)
-        at_stage(1, lambda j: ring("d1", j, 1))
-        at_stage(0, d_begin)
+        either(4, d_turn2)
+        either(3, lambda name, j: ring(name + "2", j, 1))
+        either(2, d_turn)
+        either(1, lambda name, j: ring(name + "1", j, 1))
+        either(0, d_begin)
         return carry
 
     lax.fori_loop(0, total + LAG * (nz // 2 + 4), tick, 0)
@@ -561,7 +548,7 @@
             dma((3, SLOTS)),
             [(dma((n // 2, SLOTS, 2)), dma((n // 2, SLOTS, 2))) for n in steps],
         ],
-        compiler_params=pltpu.CompilerParams(vmem_limit_bytes=VMEM_LIMIT, collective_id=1, has_side_effects=True),
+        compiler_params=pltpu.CompilerParams(vmem_limit_bytes=GATHER_VMEM, collective_id=1, has_side_effects=True),
         name="gather",
     )(ng, nu, nd)
     n = nx * ny * nz

time: 516 us -> 498 us (0.965)
  local copies, waits for them, and re-layouts: 34 us -> 24.2 us
  Pallas kernels: 476 us -> 468 us
    unnamed x19 -> x11, local copies, waits for them, and re-layouts: 34 us -> 24.2 us
    pallas_call x2 -> x1, Pallas kernels: 280 us -> 273 us  [gradients(): pl.pallas_call(reduce_kernel, grid=(chunks + total + 8 * LAG,), in_specs=...]
where the time goes in v2:
time: 498 us
  Pallas kernels  468 us (94%)
  local copies, waits for them, and re-layouts  24.2 us (5%)
    pallas_call x1, Pallas kernels, gradients(): pl.pallas_call(reduce_kernel, grid=(chunks + total + 8 * LAG,), in_specs=...  273 us
    pallas_call x1, Pallas kernels, gather(): pl.pallas_call(functools.partial(gather_kernel, JOBS), in_specs=[pl.Block...  195 us
    unnamed x11, local copies, waits for them, and re-layouts  24.2 us

profile of v2, /device:TPU:2, one launch (start us, length us, event | category | flops | bytes accessed | tf_op | source)
XLA Modules:
  0.0 498.1 jit_solution(3542012239047934335)
XLA Ops:
  0.6 0.0 copy-start.1
  0.7 0.0 copy-start.2
  0.7 0.0 copy-start.3
  0.7 273.1 %reduce.1 = (f32[2,4,8192]{2,1,0:T(4,128)}, f32[2,4,8192]{2,1,0:T(4,128)}, f32[2,64,512]{2,1,0:T(8,128)}) custom-call(bf16[1024,512]{1,0:T(8,128)(2,1)} %bitcast.8, bf16[1024,512]{1,0:T(8,128)(2,1)} %bitcast.9, bf16[2,512,8192]{2,1,0:T(8,128)(2,1)} %wg.1, bf16[2,512,8192]{2,1,0:T(8,128)(2,1)} %wu.1, bf16[2,8192,512]{2,1,0:T(8,128)(2,1)} %wd.1), custom_call_target="tpu_custom_call" | custom-call | tf_op jit(solution)/shard_map/reduce/pallas_call | solution.py:379
  273.8 0.0 copy-done.1
  273.8 0.0 copy-done.2
  273.8 2.0 fusion.8
  275.8 0.0 copy-done.3
  275.8 3.0 fusion.2
  278.8 195.2 %gather.1 = (bf16[2,4,4,32,8192]{4,3,2,1,0:T(8,128)(2,1)S(1)}, bf16[2,4,4,32,8192]{4,3,2,1,0:T(8,128)(2,1)S(1)}, bf16[2,4,4,8,64,512]{5,4,3,2,1,0:T(8,128)(2,1)}) custom-call(bf16[2,4,8192]{2,1,0:T(4,128)(2,1)S(1)} %get-tuple-element.27.ng, bf16[2,4,8192]{2,1,0:T(4,128)(2,1)S(1)} %get-tuple-element.30.nu, bf16[2,64,512]{2,1,0:T(8,128)(2,1)S(1)} %get-tuple-element.21.nd), custom_call_target="tpu_custom_call" | custom-call | tf_op jit(solution)/shard_map/gather/pallas_call | solution.py:540
  474.0 6.2 %copy.23 = bf16[2,512,8192]{2,1,0:T(8,128)(2,1)} copy(bf16[2,512,8192]{2,1,0:T(8,128)(2,1)S(1)} %bitcast.6) | data formatting | bytes 33554432
  480.1 0.0 copy-start
  480.1 8.5 %copy.24 = bf16[2,512,8192]{2,1,0:T(8,128)(2,1)} copy(bf16[2,512,8192]{2,1,0:T(8,128)(2,1)S(1)} %bitcast.5) | data formatting | bytes 33554432
  488.6 3.3 copy-done
  492.0 6.2 %copy.25 = bf16[2,8192,512]{2,1,0:T(8,128)(2,1)} copy(bf16[2,8192,512]{2,1,0:T(8,128)(2,1)S(1)} %bitcast.7) | data formatting | bytes 33554432
Async XLA Ops:
  0.6 273.1 %copy-start.1 = (f32[2,64,512]{2,1,0:T(8,128)S(1)}, f32[2,64,512]{2,1,0:T(8,128)}, u32[]{:S(2)}) copy-start(f32[2,64,512]{2,1,0:T(8,128)} %param.21) | copy-start | bytes 786436
  0.7 273.1 %copy-start.2 = (f32[2,64,512]{2,1,0:T(8,128)S(1)}, f32[2,64,512]{2,1,0:T(8,128)}, u32[]{:S(2)}) copy-start(f32[2,64,512]{2,1,0:T(8,128)} %param.18) | copy-start | bytes 786436
  0.7 275.1 %copy-start.3 = (f32[2,4,8192]{2,1,0:T(4,128)S(1)}, f32[2,4,8192]{2,1,0:T(4,128)}, u32[]{:S(2)}) copy-start(f32[2,4,8192]{2,1,0:T(4,128)} %param.19) | copy-start | bytes 786436
  480.1 11.8 %copy-start = (bf16[2,4,4,8,64,512]{5,4,3,2,1,0:T(8,128)(2,1)S(1)}, bf16[2,4,4,8,64,512]{5,4,3,2,1,0:T(8,128)(2,1)}, u32[]{:S(2)}) copy-start(bf16[2,4,4,8,64,512]{5,4,3,2,1,0:T(8,128)(2,1)} %get-tuple-element.20) | copy-start | bytes 50331652

commit v3 on v2

--- a/solution.py
+++ b/solution.py
@@ -14,7 +14,9 @@
 GATHER_VMEM = 12 << 20
 LAG = 2
 SLOTS = 6
-JOBS = 8
+GROUPS = 3
+JOBS = 4
+GATHER_LAG = 3
 
 
 def dot(a, b, dims=((1,), (0,))):
@@ -102,8 +104,8 @@
 
 def reduce_kernel(x, dy, wg, wu, wd, out_g, out_u, out_d, *scratch):
     (hid, dgate, dup, da, dh, a_all, at_all, h1,
-     own_g, own_u, own_d, acc_g2, acc_u2, acc_g3, acc_u3, acc_d2, acc_d3,
-     rg, ru, rd, sg, su, sd, sems) = scratch
+     own_g, own_u, own_d, acc_g2, acc_u2, acc_w3, acc_d2, acc_d3,
+     rg, ru, rw, rd, sg, su, sw, sd, sems) = scratch
     nx, ny, nz = GRID
     chunks = nx * ny
     total = 2 * chunks
@@ -115,21 +117,15 @@
     senders = {
         name: Sender(axis, at, neighbour, *sem)
         for (name, axis), sem in zip(
-            (("g1", 0), ("g2", 1), ("g3", 2), ("u1", 1), ("u2", 0), ("u3", 2), ("d1", 2), ("d2", 1), ("d3", 0)), sems, strict=True
+            (("g1", 0), ("g2", 1), ("u1", 1), ("u2", 0), ("w3", 2), ("d1", 2), ("d2", 1), ("d3", 0)), sems, strict=True
         )
     }
 
     def halves(array, ref):
-        if array in ("g1", "g2", "d1", "d2", "d3"):
-            h = ref.shape[-2] // 2
-            return ref.at[pl.ds(0, h)], ref.at[pl.ds(h, h)]
-        if array == "u1":
-            return ref.at[pl.ds(0, nx // 2)], ref.at[pl.ds(nx // 2, nx // 2)]
-        if array == "u2":
-            h = ref.shape[-2] // 2
-            return ref.at[pl.ds(0, h)], ref.at[pl.ds(h, h)]
-        h = ref.shape[-1] // 2
-        return ref.at[:, pl.ds(0, h)], ref.at[:, pl.ds(h, h)]
+        if array == "w3":
+            return ref.at[0], ref.at[1]
+        h = ref.shape[0] // 2
+        return ref.at[pl.ds(0, h)], ref.at[pl.ds(h, h)]
 
     def first(array, slot, own, recv):
         s = senders[array]
@@ -189,9 +185,6 @@
 
         return run
 
-    def columns(c):
-        return pl.ds(pl.multiple_of(lax.rem(c, chunks) * f, f), f)
-
     def layer_of(c):
         return 1 - lax.div(c, chunks)
 
@@ -224,7 +217,21 @@
             up = dot(a_all[0, s], wu[0])
             da[s] += dot((gate * jax.nn.sigmoid(gate) * up).astype(BF), wd[0])
 
-    def wide(which, own, acc2, acc3, recv, stage, out):
+    def w3(c):
+        slot = lax.rem(lax.div(c, ny), GROUPS)
+        return later("w3", slot, lambda q: acc_w3.at[slot, q], rw, sw)
+
+    def w_end(c):
+        done = w3(c)[2]()
+        cols = pl.ds(pl.multiple_of(lax.div(lax.rem(c, chunks), ny) * (ny * f), ny * f), ny * f)
+        out_g[layer_of(c), :, cols] = done[0]
+        out_u[layer_of(c), :, cols] = done[1]
+
+    at_stage(8, ny)(w_end)
+    for j in (3, 2, 1):
+        at_stage(4 + j, ny)(lambda c, j=j: w3(c)[1](j))
+
+    def wide(which, own, acc2, recv, stage):
         def own1(slot):
             return (lambda q: own.at[slot, q]) if which == "g" else (lambda q: own.at[slot, :, q])
 
@@ -236,23 +243,12 @@
             slot = lax.rem(c, SLOTS)
             return later(which + "2", slot, lambda q: acc2.at[slot, q], recv[2:4], stage[0:2])
 
-        def p3(c):
-            slot, long = lax.rem(c, SLOTS), lax.rem(c, 2 * SLOTS)
-            return later(which + "3", slot, lambda q: acc3.at[long, q], recv[4:8], stage[2:6])
-
-        def end(c):
-            out[layer_of(c), :, columns(c)] = p3(c)[2]()
-
-        at_stage(8)(end)
-        for j in (3, 2, 1):
-            at_stage(4 + j)(lambda c, j=j: p3(c)[1](j))
-
         def turn2(c):
             done = p2(c)[2]()
-            rows = acc3.shape[2]
+            rows = acc_w3.shape[3]
+            cols = pl.ds(pl.multiple_of(lax.rem(c, ny) * f, f), f)
             for q in range(nz):
-                acc3[lax.rem(c, 2 * SLOTS), q] = done[q * rows:(q + 1) * rows]
-            p3(c)[0]()
+                acc_w3[lax.rem(lax.div(c, ny), GROUPS), q, "gu".index(which), :, cols] = done[q * rows:(q + 1) * rows]
 
         at_stage(4)(turn2)
         at_stage(3)(lambda c: p2(c)[1](1))
@@ -265,8 +261,9 @@
         at_stage(2)(turn1)
         at_stage(1)(lambda c: p1(c)[1](1))
 
-    wide("g", own_g, acc_g2, acc_g3, rg, sg, out_g)
-    wide("u", own_u, acc_u2, acc_u3, ru, su, out_u)
+    wide("g", own_g, acc_g2, rg, sg)
+    wide("u", own_u, acc_u2, ru, su)
+    at_stage(4, ny)(lambda c: w3(c)[0]())
 
     def d1(c):
         slot, long = lax.rem(c, SLOTS), lax.rem(c, 2 * SLOTS)
@@ -346,17 +343,16 @@
         return layer, c, 0
 
     s, long = SLOTS, 2 * SLOTS
-    g_blocks = [((ny * nz * rg) // 2, f), (ny * nz * rg, f), (nz * rg // 2, f), (nz * rg, f), (rg, f // 2), (rg, f), (rg, f), (rg, f)]
-    u_blocks = [(nx // 2, nz * rg, f), (nx, nz * rg, f), (nz * rg // 2, f), (nz * rg, f), (rg, f // 2), (rg, f), (rg, f), (rg, f)]
-    if nz == 4:
-        g_blocks, u_blocks = g_blocks[:6], u_blocks[:6]
+    g_blocks = [((ny * nz * rg) // 2, f), (ny * nz * rg, f), (nz * rg // 2, f), (nz * rg, f)]
+    u_blocks = [(nx // 2, nz * rg, f), (nx, nz * rg, f), (nz * rg // 2, f), (nz * rg, f)]
+    w_blocks = [(rg, ny * f)] + [(2, rg, ny * f)] * (nz // 2 - 1)
     d_blocks = [(rd // 2, d)] + [(rd, d)] * (nz // 2 - 1) + [(rd // 2, d), (rd, d)] * 2
     d_slots = [s] * (nz // 2) + [2] * 4
-    steps = {"g1": nx, "g2": ny, "g3": nz, "u1": ny, "u2": nx, "u3": nz, "d1": nz, "d2": ny, "d3": nx}
+    steps = {"g1": nx, "g2": ny, "u1": ny, "u2": nx, "w3": nz, "d1": nz, "d2": ny, "d3": nx}
     dma = pltpu.SemaphoreType.DMA
 
     def sems(name, n):
-        count = 2 if name in ("d2", "d3") else s
+        count = {"d2": 2, "d3": 2, "w3": GROUPS}.get(name, s)
         return (dma((n // 2, count, 2)), dma((n // 2, count, 2)))
 
     scratch = [
@@ -365,13 +361,15 @@
         pltpu.VMEM((2, tokens, d), BF), pltpu.VMEM((2, d, tokens), BF), pltpu.VMEM((tokens, d), BF),
         pltpu.VMEM((s, nx, ny * nz * rg, f), BF), pltpu.VMEM((s, nx, ny, nz * rg, f), BF), pltpu.VMEM((long, nz, rd, d), BF),
         pltpu.VMEM((s, ny, nz * rg, f), F32), pltpu.VMEM((s, nx, nz * rg, f), F32),
-        pltpu.VMEM((long, nz, rg, f), F32), pltpu.VMEM((long, nz, rg, f), F32),
+        pltpu.VMEM((GROUPS, nz, 2, rg, ny * f), F32),
         pltpu.VMEM((2, ny, rd, d), F32), pltpu.VMEM((2, nx, rd, d), F32),
         [pltpu.VMEM((s, 2, *b), BF) for b in g_blocks],
         [pltpu.VMEM((s, 2, *b), BF) for b in u_blocks],
+        [pltpu.VMEM((GROUPS, 2, *b), BF) for b in w_blocks],
         [pltpu.VMEM((k, 2, *b), BF) for k, b in zip(d_slots, d_blocks, strict=True)],
         [pltpu.VMEM((s, 2, *b), BF) for b in g_blocks[2:]],
         [pltpu.VMEM((s, 2, *b), BF) for b in u_blocks[2:]],
+        [pltpu.VMEM((GROUPS, 2, *b), BF) for b in w_blocks],
         [pltpu.VMEM((k, 2, *b), BF) for k, b in zip(d_slots[nz // 2:], d_blocks[nz // 2:], strict=True)],
         [sems(name, n) for name, n in steps.items()],
     ]
@@ -410,7 +408,7 @@
         layer, q = piece(j)
         cols = pl.ds(pl.multiple_of(q * f, f), f)
         rows = pl.ds(pl.multiple_of(q * r, r), r)
-        zs = lax.rem(j, 2 * SLOTS)
+        zs = j
         left, right = pl.ds(0, nd.shape[2] // 2), pl.ds(nd.shape[2] // 2, nd.shape[2] // 2)
         h = nz * ng.shape[1] // 2
         return {
@@ -428,7 +426,7 @@
         }[name]
 
     def ring(name, j, i, first=None):
-        slot = lax.rem(j, SLOTS)
+        slot = j
         s = senders[name]
         full, half = blocks(name, j, slot)
         if i > 0:
@@ -439,7 +437,7 @@
             s.copy(i, slot, d, first if first is not None else dst, dst).start()
 
     def arrived(name, j, i):
-        slot = lax.rem(j, SLOTS)
+        slot = j
         s = senders[name]
         full, half = blocks(name, j, slot)
         refs = []
@@ -450,26 +448,26 @@
 
     def tick(t, carry):
         def at_stage(k, fn):
-            j = t - LAG * k
+            j = t - GATHER_LAG * k
             pl.when((j >= 0) & (j < total))(lambda: fn(j))
 
         def wide(which, new, zb, yb, which_local):
             p1, p2, p3 = (which + k for k in "123")
 
             def keep(j):
-                slot = lax.rem(j, SLOTS)
+                slot = j
                 own = blocks(p2, j, slot)[0](y_ if which == "g" else x_)
                 return pltpu.make_async_copy(yb.at[slot], own, local.at[which_local, slot])
 
             def begin(j):
                 layer, q = piece(j)
-                zb[lax.rem(j, 2 * SLOTS), z_] = new[layer, :, pl.ds(pl.multiple_of(q * f, f), f)]
+                zb[j, z_] = new[layer, :, pl.ds(pl.multiple_of(q * f, f), f)]
                 ring(p1, j, 0)
 
             def turn(j):
-                slot = lax.rem(j, SLOTS)
+                slot = j
                 arrived(p1, j, nz // 2 - 1)
-                yb[slot] = zb[lax.rem(j, 2 * SLOTS)].reshape(yb.shape[1:])
+                yb[slot] = zb[j].reshape(yb.shape[1:])
                 keep(j).start()
                 ring(p2, j, 0, yb.at[slot])
 
@@ -492,7 +490,7 @@
         wide("u", nu, zu, yu, 1)
 
         def keep(j):
-            slot = lax.rem(j, SLOTS)
+            slot = j
             layer, q = piece(j)
             own = nd.at[layer, pl.ds(pl.multiple_of(q * r, r), r)]
             return own, pltpu.make_async_copy(own, blocks("d1", j, slot)[0](x_), local.at[2, slot])
@@ -526,7 +524,7 @@
         either(0, d_begin)
         return carry
 
-    lax.fori_loop(0, total + LAG * (nz // 2 + 4), tick, 0)
+    lax.fori_loop(0, total + GATHER_LAG * (nz // 2 + 4), tick, 0)
 
 
 def gather(ng, nu, nd):
@@ -543,10 +541,10 @@
         out_specs=[pl.BlockSpec(memory_space=pl.ANY)] * 3,
         out_shape=[wide, wide, jax.ShapeDtypeStruct((2, nx, ny, nz, rd, d), BF)],
         scratch_shapes=[
-            pltpu.VMEM((2 * SLOTS, nz, rg, f), BF), pltpu.VMEM((2 * SLOTS, nz, rg, f), BF),
-            pltpu.VMEM((SLOTS, nz * rg, f), BF), pltpu.VMEM((SLOTS, nz * rg, f), BF),
-            dma((3, SLOTS)),
-            [(dma((n // 2, SLOTS, 2)), dma((n // 2, SLOTS, 2))) for n in steps],
+            pltpu.VMEM((2 * JOBS, nz, rg, f), BF), pltpu.VMEM((2 * JOBS, nz, rg, f), BF),
+            pltpu.VMEM((2 * JOBS, nz * rg, f), BF), pltpu.VMEM((2 * JOBS, nz * rg, f), BF),
+            dma((3, 2 * JOBS)),
+            [(dma((n // 2, 2 * JOBS, 2)), dma((n // 2, 2 * JOBS, 2))) for n in steps],
         ],
         compiler_params=pltpu.CompilerParams(vmem_limit_bytes=GATHER_VMEM, collective_id=1, has_side_effects=True),
         name="gather",

time: 498 us -> 492 us (0.988)
  Pallas kernels: 468 us -> 462 us
where the time goes in v3:
time: 492 us
  Pallas kernels  462 us (94%)
  local copies, waits for them, and re-layouts  24.2 us (5%)
  other arithmetic  4.96 us (1%)
    pallas_call x1, Pallas kernels, gradients(): pl.pallas_call(reduce_kernel, grid=(chunks + total + 8 * LAG,), in_specs=...  271 us
    pallas_call x1, Pallas kernels, gather(): pl.pallas_call(functools.partial(gather_kernel, JOBS), in_specs=[pl.Block...  192 us
    unnamed x11, local copies, waits for them, and re-layouts  24.2 us

profile of v3, /device:TPU:2, one launch (start us, length us, event | category | flops | bytes accessed | tf_op | source)
XLA Modules:
  0.0 492.2 jit_solution(8759880688118018755)
XLA Ops:
  0.6 0.0 copy-start.1
  0.7 0.0 copy-start.2
  0.7 0.0 copy-start.3
  0.7 270.7 %reduce.1 = (f32[2,4,8192]{2,1,0:T(4,128)}, f32[2,4,8192]{2,1,0:T(4,128)}, f32[2,64,512]{2,1,0:T(8,128)}) custom-call(bf16[1024,512]{1,0:T(8,128)(2,1)} %bitcast.8, bf16[1024,512]{1,0:T(8,128)(2,1)} %bitcast.9, bf16[2,512,8192]{2,1,0:T(8,128)(2,1)} %wg.1, bf16[2,512,8192]{2,1,0:T(8,128)(2,1)} %wu.1, bf16[2,8192,512]{2,1,0:T(8,128)(2,1)} %wd.1), custom_call_target="tpu_custom_call" | custom-call | tf_op jit(solution)/shard_map/reduce/pallas_call | solution.py:377
  271.4 0.0 copy-done.1
  271.4 0.0 copy-done.2
  271.5 2.0 fusion.8
  273.4 0.0 copy-done.3
  273.4 3.0 fusion.2
  276.4 191.6 %gather.1 = (bf16[2,4,4,32,8192]{4,3,2,1,0:T(8,128)(2,1)S(1)}, bf16[2,4,4,32,8192]{4,3,2,1,0:T(8,128)(2,1)S(1)}, bf16[2,4,4,8,64,512]{5,4,3,2,1,0:T(8,128)(2,1)}) custom-call(bf16[2,4,8192]{2,1,0:T(4,128)(2,1)S(1)} %get-tuple-element.27.ng, bf16[2,4,8192]{2,1,0:T(4,128)(2,1)S(1)} %get-tuple-element.30.nu, bf16[2,64,512]{2,1,0:T(8,128)(2,1)S(1)} %get-tuple-element.21.nd), custom_call_target="tpu_custom_call" | custom-call | tf_op jit(solution)/shard_map/gather/pallas_call | solution.py:538
  468.1 6.2 %copy.23 = bf16[2,512,8192]{2,1,0:T(8,128)(2,1)} copy(bf16[2,512,8192]{2,1,0:T(8,128)(2,1)S(1)} %bitcast.6) | data formatting | bytes 33554432
  474.2 0.0 copy-start
  474.2 8.5 %copy.24 = bf16[2,512,8192]{2,1,0:T(8,128)(2,1)} copy(bf16[2,512,8192]{2,1,0:T(8,128)(2,1)S(1)} %bitcast.5) | data formatting | bytes 33554432
  482.7 3.3 copy-done
  486.0 6.2 %copy.25 = bf16[2,8192,512]{2,1,0:T(8,128)(2,1)} copy(bf16[2,8192,512]{2,1,0:T(8,128)(2,1)S(1)} %bitcast.7) | data formatting | bytes 33554432
Async XLA Ops:
  0.6 270.8 %copy-start.1 = (f32[2,64,512]{2,1,0:T(8,128)S(1)}, f32[2,64,512]{2,1,0:T(8,128)}, u32[]{:S(2)}) copy-start(f32[2,64,512]{2,1,0:T(8,128)} %param.21) | copy-start | bytes 786436
  0.7 270.8 %copy-start.2 = (f32[2,64,512]{2,1,0:T(8,128)S(1)}, f32[2,64,512]{2,1,0:T(8,128)}, u32[]{:S(2)}) copy-start(f32[2,64,512]{2,1,0:T(8,128)} %param.18) | copy-start | bytes 786436
  0.7 272.7 %copy-start.3 = (f32[2,4,8192]{2,1,0:T(4,128)S(1)}, f32[2,4,8192]{2,1,0:T(4,128)}, u32[]{:S(2)}) copy-start(f32[2,4,8192]{2,1,0:T(4,128)} %param.19) | copy-start | bytes 786436
  474.2 11.8 %copy-start = (bf16[2,4,4,8,64,512]{5,4,3,2,1,0:T(8,128)(2,1)S(1)}, bf16[2,4,4,8,64,512]{5,4,3,2,1,0:T(8,128)(2,1)}, u32[]{:S(2)}) copy-start(bf16[2,4,4,8,64,512]{5,4,3,2,1,0:T(8,128)(2,1)} %get-tuple-element.20) | copy-start | bytes 50331652

commit v4 on v3

v4 whole, which is shorter than its diff:
```python
import functools

import jax
import jax.numpy as jnp
from jax import lax
from jax.experimental import pallas as pl
from jax.experimental.pallas import tpu as pltpu
from jax.sharding import PartitionSpec as P

GRID = (4, 4, 8)
BF, F32 = jnp.bfloat16, jnp.float32
MESH = pl.DeviceIdType.MESH
VMEM_LIMIT = 66_000_000
GATHER_VMEM = 12 << 20
LAG = 2
SLOTS = 6
GROUPS = 3
JOBS = 4


def dot(a, b, dims=((1,), (0,))):
    return lax.dot_general(a, b, (dims, ((), ())), preferred_element_type=F32)


def normed(h):
    wide = h.astype(F32)
    scale = lax.rsqrt(jnp.mean(wide**2, -1, keepdims=True) + 1e-6)
    return (wide * scale).astype(BF)


def place():
    nx, ny, nz = GRID
    me = lax.axis_index("dp")
    at = (lax.div(me, ny * nz), lax.rem(lax.div(me, nz), ny), lax.rem(me, nz))

    def neighbour(axis, step):
        c = list(at)
        c[axis] = lax.rem(at[axis] + (step + GRID[axis]), GRID[axis])
        return (c[0] * ny + c[1]) * nz + c[2]

    return at, neighbour


def greet(neighbour, whole):
    steps = [(axis, step) for axis in range(3) for step in (range(1, GRID[axis]) if whole else (1, GRID[axis] - 1))]
    for axis, step in steps:
        pl.semaphore_signal(pltpu.get_barrier_semaphore(), inc=1, device_id={"dp": neighbour(axis, step)}, device_id_type=MESH)
    return len(steps)


class Sender:
    def __init__(self, axis, at, neighbour, send, recv):
        self.n, self.p = GRID[axis], at[axis]
        self.to = (neighbour(axis, 1), neighbour(axis, -1))
        self.send, self.recv = send, recv

    def block(self, step):
        return lax.rem(self.p + (step + self.n), self.n)

    def copy(self, step, slot, d, src, dst):
        return pltpu.make_async_remote_copy(
            src_ref=src, dst_ref=dst, send_sem=self.send.at[step, slot], recv_sem=self.recv.at[step, slot],
            device_id={"dp": self.to[d]}, device_id_type=MESH,
        )

    def wait(self, step, slot, both):
        for sem in (self.recv, self.send):
            pltpu.make_async_copy(both, both, sem.at[step, slot]).wait()


class Direct:
    def __init__(self, axis, at, neighbour, own, stage, recv, send_sem, recv_sem):
        n, p = GRID[axis], at[axis]
        self.own, self.mine = own, p
        self.copies = []
        for q in range(1, n):
            copy = pltpu.make_async_remote_copy(
                src_ref=stage.at[q - 1], dst_ref=recv.at[q - 1], send_sem=send_sem.at[q - 1], recv_sem=recv_sem.at[q - 1],
                device_id={"dp": neighbour(axis, q)}, device_id_type=MESH,
            )
            self.copies.append((lax.rem(p + q, n), stage.at[q - 1], recv.at[q - 1], copy))

    def start(self):
        for block, stage, _, copy in self.copies:
            stage[...] = self.own(block)[...].astype(BF)
            copy.start()

    def finish(self):
        done = self.own(self.mine)[...]
        for _, _, recv, copy in self.copies:
            copy.wait_recv()
            copy.wait_send()
            done = done + recv[...].astype(F32)
        return done


def compute(layer, blocks, a_all, at_all, dh, wg, wu, wd, hid, dgate, dup, da):
    tokens = dgate.shape[0]
    rows = tokens // blocks
    for b in range(blocks):
        s = pl.ds(b * rows, rows)
        a = a_all[layer, s]
        gate = dot(a, wg)
        up = dot(a, wu)
        ct = dot(dh[layer, s], wd, ((1,), (1,))).astype(BF).astype(F32)
        sig = jax.nn.sigmoid(gate)
        silu = gate * sig
        hid[s] = (silu * up).astype(BF)
        dup[s] = (ct * silu).astype(BF)
        dgate[s] = (ct * up * (sig + silu * (1.0 - sig))).astype(BF)

    if layer == 1:
        da[...] += dot(dgate[...], wg, ((1,), (1,))) + dot(dup[...], wu, ((1,), (1,)))

    at = at_all[layer]
    return dot(at, dgate[...]), dot(at, dup[...]), dot(hid[...], dh[layer], ((0,), (0,)))


def reduce_kernel(x, dy, wg, wu, wd, out_g, out_u, out_d, *scratch):
    (hid, dgate, dup, da, dh, a_all, at_all, h1,
     own_g, own_u, own_d, acc_g2, acc_u2, acc_w3, acc_d2, acc_d3,
     rg, ru, rw, rd, sg, su, sw, sd, sems, direct, hold_g, hold_u, hold_d, hold_sem) = scratch
    nx, ny, nz = GRID
    chunks = nx * ny
    total = 2 * chunks
    f = hold_g.shape[2]
    at, neighbour = place()

    senders = {
        name: Sender(axis, at, neighbour, *sem)
        for (name, axis), sem in zip(
            (("g1", 0), ("g2", 1), ("u1", 1), ("u2", 0), ("w3", 2), ("d1", 2), ("d2", 1), ("d3", 0)), sems, strict=True
        )
    }

    def halves(array, ref):
        if array == "w3":
            return ref.at[0], ref.at[1]
        h = ref.shape[0] // 2
        return ref.at[pl.ds(0, h)], ref.at[pl.ds(h, h)]

    def first(array, slot, own, recv):
        s = senders[array]

        def start():
            for d, half in enumerate(halves(array, own(s.block(s.n // 2)))):
                s.copy(0, slot, d, half, recv[0].at[slot, d]).start()

        def middle(j):
            s.wait(j - 1, slot, recv[j - 1].at[slot])
            q = s.n // 2 - j
            for d in (0, 1):
                block = own(s.block(q if d == 0 else -q))
                into = halves(array, block)[d] if j == 1 else block
                into[...] = (into[...].astype(F32) + recv[j - 1][slot, d].astype(F32)).astype(BF)
                s.copy(j, slot, d, block, recv[j].at[slot, d]).start()

        def last():
            j = s.n // 2
            s.wait(j - 1, slot, recv[j - 1].at[slot])
            return own(s.p)[...].astype(F32) + recv[j - 1][slot, 0].astype(F32) + recv[j - 1][slot, 1].astype(F32)

        return start, middle, last

    def later(array, slot, own, recv, stage):
        s = senders[array]

        def start():
            for d, half in enumerate(halves(array, own(s.block(s.n // 2)))):
                stage[0][slot, d] = half[...].astype(BF)
                s.copy(0, slot, d, stage[0].at[slot, d], recv[0].at[slot, d]).start()

        def middle(j):
            s.wait(j - 1, slot, recv[j - 1].at[slot])
            q = s.n // 2 - j
            for d in (0, 1):
                block = own(s.block(q if d == 0 else -q))
                into = halves(array, block)[d] if j == 1 else block
                into[...] = into[...] + recv[j - 1][slot, d].astype(F32)
                stage[j][slot, d] = block[...].astype(BF)
                s.copy(j, slot, d, stage[j].at[slot, d], recv[j].at[slot, d]).start()

        def last():
            j = s.n // 2
            s.wait(j - 1, slot, recv[j - 1].at[slot])
            return own(s.p)[...] + recv[j - 1][slot, 0].astype(F32) + recv[j - 1][slot, 1].astype(F32)

        return start, middle, last

    def layer_of(c):
        return 1 - lax.div(c, chunks)

    def enter(layer, h):
        a = normed(h)
        a_all[layer] = a
        at_all[layer] = a.T

    def begin():
        enter(0, x[...])
        dh[1] = dy[...]
        da[...] = jnp.zeros_like(da)

    def between():
        h = x[...] + da[...].astype(BF)
        h1[...] = h
        enter(1, h)
        da[...] = jnp.zeros_like(da)

    def weights(i, act):
        slot, layer = lax.rem(i, 2), lax.rem(lax.div(i, chunks), 2)
        part = pl.ds(pl.multiple_of(lax.rem(i, chunks) * f, f), f)
        for k, (src, dst) in enumerate(((wg.at[layer, :, part], hold_g), (wu.at[layer, :, part], hold_u), (wd.at[layer, part], hold_d))):
            act(pltpu.make_async_copy(src, dst.at[slot], hold_sem.at[slot, k]))

    def next_weights(i):
        weights(i, lambda c: c.wait())
        pl.when(i + 1 < 3 * chunks)(lambda: weights(i + 1, lambda c: c.start()))
        slot = lax.rem(i, 2)
        return hold_g[slot], hold_u[slot], hold_d[slot]

    def forward(i):
        g, u, d = next_weights(i)
        rows = hid.shape[0] // 2
        for b in range(2):
            s = pl.ds(b * rows, rows)
            gate = dot(a_all[0, s], g)
            up = dot(a_all[0, s], u)
            da[s] += dot((gate * jax.nn.sigmoid(gate) * up).astype(BF), d)

    def exchange(t):
        rings(t, lambda k, every, keep: stage(t, k, every, keep))

    def stage(t, k, every, keep):
        def run(fn):
            c = t - LAG * k
            on = (c >= 0) & (c < total)
            if every > 1:
                on &= lax.rem(c, every) == every - 1
            if keep is not None:
                on &= (c < total - 1) if keep == "early" else (c == total - 1)
            pl.when(on)(functools.partial(fn, c))

        return run

    def rings(t, at_point):
        def at_stage(k, every=1, keep=None):
            return at_point(k, every, keep)

        def d1(c):
            slot, long = lax.rem(c, SLOTS), lax.rem(c, 2 * SLOTS)
            return first("d1", slot, lambda q: own_d.at[long, q], rd[0:4])

        def d2(c):
            slot = lax.rem(lax.div(c, ny), 2)
            return later("d2", slot, lambda q: acc_d2.at[slot, q], rd[4:6], sd[0:2])

        def d3(c):
            slot = layer_of(c)
            return later("d3", slot, lambda q: acc_d3.at[slot, q], rd[6:8], sd[2:4])

        def d2_direct():
            slot = ((total - 1) // ny) % 2
            return Direct(1, at, neighbour, lambda q: acc_d2.at[slot, q], *direct[1])

        def d3_direct():
            return Direct(0, at, neighbour, lambda q: acc_d3.at[0, q], *direct[2])

        def d_last1(c):
            acc_d3[0, nx - 1] = d2_direct().finish()
            d3_direct().start()

        def d_last2(c):
            out_d[0] = d3_direct().finish()

        def d_end(c):
            out_d[layer_of(c)] = d3(c)[2]()

        def d_turn2(c):
            acc_d3[layer_of(c), lax.rem(lax.div(c, ny), nx)] = d2(c)[2]()

        def d_turn1(c):
            acc_d2[lax.rem(lax.div(c, ny), 2), lax.rem(c, ny)] = d1(c)[2]()

        at_stage(8, chunks, "early")(d_end)
        at_stage(7, chunks, "early")(lambda c: d3(c)[1](1))
        at_stage(6, ny, "early")(d_turn2)
        at_stage(6, chunks, "early")(lambda c: d3(c)[0]())
        at_stage(5, ny, "early")(lambda c: d2(c)[1](1))
        at_stage(6, ny, "last")(d_last2)
        at_stage(5, ny, "last")(d_last1)
        at_stage(4)(d_turn1)
        at_stage(4, ny, "early")(lambda c: d2(c)[0]())
        at_stage(4, ny, "last")(lambda c: d2_direct().start())
        for j in (3, 2, 1):
            at_stage(j)(lambda c, j=j: d1(c)[1](j))

        def w3(c):
            slot = lax.rem(lax.div(c, ny), GROUPS)
            return later("w3", slot, lambda q: acc_w3.at[slot, q], rw, sw)

        def w_direct():
            slot = ((total - 1) // ny) % GROUPS
            return Direct(2, at, neighbour, lambda q: acc_w3.at[slot, q], *direct[0])

        def w_end(c, last=False):
            done = w_direct().finish() if last else w3(c)[2]()
            cols = pl.ds(pl.multiple_of(lax.div(lax.rem(c, chunks), ny) * (ny * f), ny * f), ny * f)
            out_g[layer_of(c), :, cols] = done[0]
            out_u[layer_of(c), :, cols] = done[1]

        at_stage(8, ny, "early")(w_end)
        at_stage(5, ny, "last")(lambda c: w_end(c, True))
        for j in (3, 2, 1):
            at_stage(4 + j, ny, "early")(lambda c, j=j: w3(c)[1](j))

        def wide(which, own, acc2, recv, stage):
            def own1(slot):
                return (lambda q: own.at[slot, q]) if which == "g" else (lambda q: own.at[slot, :, q])

            def p1(c):
                slot = lax.rem(c, SLOTS)
                return first(which + "1", slot, own1(slot), recv[0:2])

            def p2(c):
                slot = lax.rem(c, SLOTS)
                return later(which + "2", slot, lambda q: acc2.at[slot, q], recv[2:4], stage[0:2])

            def turn2(c):
                done = p2(c)[2]()
                rows = acc_w3.shape[3]
                cols = pl.ds(pl.multiple_of(lax.rem(c, ny) * f, f), f)
                for q in range(nz):
                    acc_w3[lax.rem(lax.div(c, ny), GROUPS), q, "gu".index(which), :, cols] = done[q * rows:(q + 1) * rows]

            at_stage(4)(turn2)
            at_stage(3)(lambda c: p2(c)[1](1))

            def turn1(c):
                done = p1(c)[2]()
                acc2[lax.rem(c, SLOTS)] = done.reshape(acc2.shape[1:])
                p2(c)[0]()

            at_stage(2)(turn1)
            at_stage(1)(lambda c: p1(c)[1](1))

        wide("g", own_g, acc_g2, rg, sg)
        wide("u", own_u, acc_u2, ru, su)
        at_stage(4, ny, "early")(lambda c: w3(c)[0]())
        at_stage(4, ny, "last")(lambda c: w_direct().start())

    def backward_norm():
        h, by_a = h1[...].astype(F32), da[...].astype(BF).astype(F32)
        scale = lax.rsqrt(jnp.mean(h**2, -1, keepdims=True) + 1e-6)
        by_h = scale * by_a - h * (scale**3 * jnp.mean(by_a * h, -1, keepdims=True))
        dh[0] = dy[...] + by_h.astype(BF)

    def produce(layer, c):
        slot, long = lax.rem(c, SLOTS), lax.rem(c, 2 * SLOTS)
        g, u, d = compute(layer, 4, a_all, at_all, dh, *next_weights(chunks + c), hid, dgate, dup, da)
        own_g[slot] = g.astype(BF).reshape(own_g.shape[1:])
        own_u[slot] = u.astype(BF).reshape(own_u.shape[1:])
        own_d[long] = d.astype(BF).reshape(own_d.shape[1:])
        first("d1", slot, lambda q: own_d.at[long, q], rd[0:4])[0]()
        first("g1", slot, lambda q: own_g.at[slot, q], rg[0:2])[0]()
        first("u1", slot, lambda q: own_u.at[slot, :, q], ru[0:2])[0]()

    def ticks(start, stop, *fns):
        def tick(t, carry):
            for fn in fns:
                fn(t)
            return carry

        lax.fori_loop(start, stop, tick, 0)

    weights(0, lambda c: c.start())
    met = greet(neighbour, True)
    begin()
    ticks(0, chunks, forward)
    pl.semaphore_wait(pltpu.get_barrier_semaphore(), met)
    between()
    ticks(0, chunks, exchange, functools.partial(produce, 1))
    backward_norm()
    ticks(chunks, total, exchange, functools.partial(produce, 0))
    ticks(total, max(total - 1 + 6 * LAG, total - 1 - ny + 8 * LAG) + 1, exchange)


def gradients(x, dy, wg, wu, wd):
    nx, ny, nz = GRID
    n = nx * ny * nz
    tokens, d = x.shape
    ff = wg.shape[2]
    chunks = nx * ny
    f, rg, rd = ff // chunks, d // n, ff // n
    total = 2 * chunks

    s, long = SLOTS, 2 * SLOTS
    g_blocks = [((ny * nz * rg) // 2, f), (ny * nz * rg, f), (nz * rg // 2, f), (nz * rg, f)]
    u_blocks = [(nx // 2, nz * rg, f), (nx, nz * rg, f), (nz * rg // 2, f), (nz * rg, f)]
    w_blocks = [(rg, ny * f)] + [(2, rg, ny * f)] * (nz // 2 - 1)
    d_blocks = [(rd // 2, d)] + [(rd, d)] * (nz // 2 - 1) + [(rd // 2, d), (rd, d)] * 2
    d_slots = [s] * (nz // 2) + [2] * 4
    steps = {"g1": nx, "g2": ny, "u1": ny, "u2": nx, "w3": nz, "d1": nz, "d2": ny, "d3": nx}
    dma = pltpu.SemaphoreType.DMA

    def sems(name, n):
        count = {"d2": 2, "d3": 2, "w3": GROUPS}.get(name, s)
        return (dma((n // 2, count)), dma((n // 2, count)))

    scratch = [
        pltpu.VMEM((tokens, f), BF), pltpu.VMEM((tokens, f), BF), pltpu.VMEM((tokens, f), BF),
        pltpu.VMEM((tokens, d), F32), pltpu.VMEM((2, tokens, d), BF),
        pltpu.VMEM((2, tokens, d), BF), pltpu.VMEM((2, d, tokens), BF), pltpu.VMEM((tokens, d), BF),
        pltpu.VMEM((s, nx, ny * nz * rg, f), BF), pltpu.VMEM((s, nx, ny, nz * rg, f), BF), pltpu.VMEM((long, nz, rd, d), BF),
        pltpu.VMEM((s, ny, nz * rg, f), F32), pltpu.VMEM((s, nx, nz * rg, f), F32),
        pltpu.VMEM((GROUPS, nz, 2, rg, ny * f), F32),
        pltpu.VMEM((2, ny, rd, d), F32), pltpu.VMEM((2, nx, rd, d), F32),
        [pltpu.VMEM((s, 2, *b), BF) for b in g_blocks],
        [pltpu.VMEM((s, 2, *b), BF) for b in u_blocks],
        [pltpu.VMEM((GROUPS, 2, *b), BF) for b in w_blocks],
        [pltpu.VMEM((k, 2, *b), BF) for k, b in zip(d_slots, d_blocks, strict=True)],
        [pltpu.VMEM((s, 2, *b), BF) for b in g_blocks[2:]],
        [pltpu.VMEM((s, 2, *b), BF) for b in u_blocks[2:]],
        [pltpu.VMEM((GROUPS, 2, *b), BF) for b in w_blocks],
        [pltpu.VMEM((k, 2, *b), BF) for k, b in zip(d_slots[nz // 2:], d_blocks[nz // 2:], strict=True)],
        [sems(name, n) for name, n in steps.items()],
        [
            (pltpu.VMEM((n - 1, *b), BF), pltpu.VMEM((n - 1, *b), BF), dma((n - 1,)), dma((n - 1,)))
            for n, b in ((nz, (2, rg, ny * f)), (ny, (rd, d)), (nx, (rd, d)))
        ],
        pltpu.VMEM((2, d, f), BF), pltpu.VMEM((2, d, f), BF), pltpu.VMEM((2, f, d), BF), dma((2, 3)),
    ]
    vmem = pl.BlockSpec(memory_space=pltpu.VMEM)
    return pl.pallas_call(
        reduce_kernel,
        in_specs=[vmem] * 2 + [pl.BlockSpec(memory_space=pl.ANY)] * 3,
        out_specs=[vmem] * 3,
        out_shape=[jax.ShapeDtypeStruct((2, rg, ff), F32)] * 2 + [jax.ShapeDtypeStruct((2, rd, d), F32)],
        scratch_shapes=scratch,
        compiler_params=pltpu.CompilerParams(
            vmem_limit_bytes=VMEM_LIMIT, collective_id=0, has_side_effects=True
        ),
        name="reduce",
    )(x, dy, wg, wu, wd)


def gather_kernel(ng, nu, nd, og, ou, od, *scratch):
    zb, yg, yu, local, sems = scratch
    nx, ny, nz = GRID
    total = 2 * JOBS
    f, r = zb.shape[-1], nd.shape[1] // JOBS
    at, neighbour = place()
    x_, y_, z_ = at
    met = greet(neighbour, False)
    names = (("w1", 2), ("g2", 1), ("g3", 0), ("u2", 0), ("u3", 1), ("d1", 0), ("d2", 1), ("d3", 2))
    odd = (("e1", 1), ("e2", 0), ("e3", 2))
    senders = {name: Sender(axis, at, neighbour, *sem) for (name, axis), sem in zip((*names, *odd), (*sems, *sems[5:]), strict=True)}

    def piece(j):
        return 1 - lax.div(j, JOBS), lax.rem(j, JOBS)

    def blocks(name, j):
        layer, q = piece(j)
        cols, rows = pl.ds(pl.multiple_of(q * f, f), f), pl.ds(pl.multiple_of(q * r, r), r)
        h = nz * ng.shape[1] // 2
        d = nd.shape[2] // 2

        def halves(at_half, n):
            return lambda b: tuple(at_half(b, part) for part in (pl.ds(0, n), pl.ds(n, n)))

        return {
            "w1": (lambda b: zb.at[j, b], lambda b: (zb.at[j, b, 0], zb.at[j, b, 1])),
            "g2": (lambda b: og.at[layer, x_, b, :, cols], halves(lambda b, p: og.at[layer, x_, b, p, cols], h)),
            "u2": (lambda b: ou.at[layer, b, y_, :, cols], halves(lambda b, p: ou.at[layer, b, y_, p, cols], h)),
            "g3": (lambda b: og.at[layer, b, :, :, cols], halves(lambda b, p: og.at[layer, b, p, :, cols], ny // 2)),
            "u3": (lambda b: ou.at[layer, :, b, :, cols], halves(lambda b, p: ou.at[layer, p, b, :, cols], nx // 2)),
            "d1": (lambda b: od.at[layer, b, y_, z_, rows], halves(lambda b, p: od.at[layer, b, y_, z_, rows, p], d)),
            "e1": (lambda b: od.at[layer, x_, b, z_, rows], halves(lambda b, p: od.at[layer, x_, b, z_, rows, p], d)),
            "d2": (lambda b: od.at[layer, :, b, z_, rows], halves(lambda b, p: od.at[layer, p, b, z_, rows], nx // 2)),
            "e2": (lambda b: od.at[layer, b, :, z_, rows], halves(lambda b, p: od.at[layer, b, p, z_, rows], ny // 2)),
            "d3": (lambda b: od.at[layer, :, :, b, rows], halves(lambda b, p: od.at[layer, p, :, b, rows], nx // 2)),
            "e3": (lambda b: od.at[layer, :, :, b, rows], halves(lambda b, p: od.at[layer, p, :, b, rows], nx // 2)),
        }[name]

    def ring(name, j, i, first=None):
        s = senders[name]
        full, half = blocks(name, j)
        if i > 0:
            arrived(name, j, i - 1)
        for d in (0, 1):
            b = s.block(-i if d == 0 else i)
            dst = full(b) if i < s.n // 2 - 1 else half(b)[d]
            s.copy(i, lax.rem(j, SLOTS), d, first if first is not None else dst, dst).start()

    def arrived(name, j, i):
        s = senders[name]
        full = blocks(name, j)[0]
        s.wait(i, lax.rem(j, SLOTS), full(pl.ds(0, 2) if i < s.n // 2 - 1 else 0))

    def tick(t, carry):
        def at_stage(k, fn):
            j = t - LAG * k
            pl.when((j >= 0) & (j < total))(lambda: fn(j))

        def keep(which, j):
            slot = lax.rem(j, SLOTS)
            src, name, b = ((yg, "g2", y_), (yu, "u2", x_))[which]
            return pltpu.make_async_copy(src.at[slot], blocks(name, j)[0](b), local.at[which, slot])

        def begin(j):
            layer, q = piece(j)
            for k, new in enumerate((ng, nu)):
                zb[j, z_, k] = new[layer, :, pl.ds(pl.multiple_of(q * f, f), f)]
            ring("w1", j, 0)

        def turn(j):
            slot = lax.rem(j, SLOTS)
            arrived("w1", j, nz // 2 - 1)
            for which, (yb, name) in enumerate(((yg, "g2"), (yu, "u2"))):
                yb[slot] = zb[j, :, which].reshape(yb.shape[1:])
                keep(which, j).start()
                ring(name, j, 0, yb.at[slot])

        def turn2(j):
            for which, name in enumerate("gu"):
                arrived(name + "2", j, 1)
                keep(which, j).wait()
                ring(name + "3", j, 0)

        def both(fn):
            def run(j):
                for name in "gu":
                    fn(name, j)

            return run

        k = nz // 2
        at_stage(k + 4, both(lambda name, j: arrived(name + "3", j, 1)))
        at_stage(k + 3, both(lambda name, j: ring(name + "3", j, 1)))
        at_stage(k + 2, turn2)
        at_stage(k + 1, both(lambda name, j: ring(name + "2", j, 1)))
        at_stage(k, turn)
        for i in range(k - 1, 0, -1):
            at_stage(i, lambda j, i=i: ring("w1", j, i))
        at_stage(0, begin)

        def own_rows(name, j):
            layer, q = piece(j)
            own = nd.at[layer, pl.ds(pl.multiple_of(q * r, r), r)]
            return own, pltpu.make_async_copy(own, blocks(name + "1", j)[0](x_ if name == "d" else y_), local.at[2, lax.rem(j, SLOTS)])

        def d_begin(name, j):
            own, copy = own_rows(name, j)
            copy.start()
            ring(name + "1", j, 0, own)

        def d_turn(name, j):
            arrived(name + "1", j, 1)
            own_rows(name, j)[1].wait()
            ring(name + "2", j, 0)

        def d_turn2(name, j):
            arrived(name + "2", j, 1)
            ring(name + "3", j, 0)

        def either(k, fn):
            at_stage(k, lambda j: pl.when(lax.rem(j, 2) == 0)(lambda: fn("d", j)))
            at_stage(k, lambda j: pl.when(lax.rem(j, 2) == 1)(lambda: fn("e", j)))

        either(4 + k, lambda name, j: arrived(name + "3", j, k - 1))
        for i in range(k - 1, 0, -1):
            either(4 + i, lambda name, j, i=i: ring(name + "3", j, i))
        either(4, d_turn2)
        either(3, lambda name, j: ring(name + "2", j, 1))
        either(2, d_turn)
        either(1, lambda name, j: ring(name + "1", j, 1))
        either(0, d_begin)
        return carry

    pl.semaphore_wait(pltpu.get_barrier_semaphore(), met)
    lax.fori_loop(0, total + LAG * (nz // 2 + 4), tick, 0)


def gather(ng, nu, nd):
    nx, ny, nz = GRID
    _, rg, ff = ng.shape
    _, rd, d = nd.shape
    f, jobs = ff // JOBS, 2 * JOBS
    dma = pltpu.SemaphoreType.DMA
    steps = (nz, ny, nx, nx, ny, nx, ny, nz)
    wide = jax.ShapeDtypeStruct((2, nx, ny, nz * rg, ff), BF)
    got = pl.pallas_call(
        gather_kernel,
        in_specs=[pl.BlockSpec(memory_space=pltpu.VMEM)] * 3,
        out_specs=[pl.BlockSpec(memory_space=pl.ANY)] * 3,
        out_shape=[wide, wide, jax.ShapeDtypeStruct((2, nx, ny, nz, rd, d), BF)],
        scratch_shapes=[
            pltpu.VMEM((jobs, nz, 2, rg, f), BF), pltpu.VMEM((SLOTS, nz * rg, f), BF), pltpu.VMEM((SLOTS, nz * rg, f), BF),
            dma((3, SLOTS)),
            [(dma((n // 2, SLOTS)), dma((n // 2, SLOTS))) for n in steps],
        ],
        compiler_params=pltpu.CompilerParams(vmem_limit_bytes=GATHER_VMEM, collective_id=1, has_side_effects=True),
        name="gather",
    )(ng, nu, nd)
    og, ou, od = emit(*got)
    n = nx * ny * nz
    return og.reshape(2, n * rg, ff), ou.reshape(2, n * rg, ff), od.reshape(2, n * rd, d)


def emit_kernel(g, u, d, go, uo, do, hold, sems):
    copies = [pltpu.make_async_copy(a.at[i], b.at[i], sems.at[k, i]) for k, (a, b) in enumerate(((g, go), (u, uo))) for i in range(2)]
    for c in copies:
        c.start()
    pieces = [(i, x) for i in range(2) for x in range(4)]
    slots = hold.shape[0]
    ins = [pltpu.make_async_copy(d.at[p], hold.at[k % slots], sems.at[2, k]) for k, p in enumerate(pieces)]
    outs = [pltpu.make_async_copy(hold.at[k % slots], do.at[p], sems.at[3, k]) for k, p in enumerate(pieces)]
    for c in ins[:slots]:
        c.start()
    for k in range(len(pieces)):
        ins[k].wait()
        outs[k].start()
        if k >= 1 and k - 1 + slots < len(pieces):
            outs[k - 1].wait()
            ins[k - 1 + slots].start()
    for c in outs[len(pieces) - slots:] + copies:
        c.wait()


def emit(*arrays):
    return pl.pallas_call(
        emit_kernel,
        in_specs=[pl.BlockSpec(memory_space=pltpu.VMEM), pl.BlockSpec(memory_space=pltpu.VMEM), pl.BlockSpec(memory_space=pltpu.HBM)],
        out_specs=[pl.BlockSpec(memory_space=pltpu.HBM)] * 3,
        out_shape=[jax.ShapeDtypeStruct(a.shape, BF) for a in arrays],
        scratch_shapes=[pltpu.VMEM((3, *arrays[2].shape[2:]), BF), pltpu.SemaphoreType.DMA((4, 8))],
        compiler_params=pltpu.CompilerParams(vmem_limit_bytes=7 << 20),
        name="emit",
    )(*arrays)


def adamw(w, m, v, g):
    g = lax.reduce_precision(g, 8, 7)
    m = 0.9 * m + 0.1 * g
    v = 0.95 * v + 0.05 * g * g
    step = m * lax.rsqrt(v + 1e-8) + 0.1 * w
    return (w - 0.02 * step).astype(BF), m, v


def device_step(x, dy, *arrays):
    weights, ms, vs = (arrays[i:i + 3] for i in (0, 3, 6))
    sums = gradients(x[0], dy[0], *weights)
    me = lax.axis_index("dp")
    new = []
    for w, m, v, g in zip(weights, ms, vs, sums, strict=True):
        rows = m.shape[1]
        own = lax.dynamic_slice_in_dim(w, me * rows, rows, 1).astype(F32)
        new.append(adamw(own, m, v, g))
    gathered = gather(*(one[0] for one in new))
    return (*gathered, *(one[1] for one in new), *(one[2] for one in new))


def solution(mesh):
    x, w, m = P(("rep", "dp"), None, None), P(None, None, None), P(None, "dp", None)
    return jax.shard_map(
        device_step,
        mesh=mesh,
        in_specs=(x, x, w, w, w, *[m] * 6),
        out_specs=(*[P("rep", None, None)] * 3, *[P("rep", "dp", None)] * 6),
        check_vma=False,
    )
```

time: 492 us -> 480 us (0.976)
  local copies, waits for them, and re-layouts: 24.2 us -> 0.01 us
  Pallas kernels: 462 us -> 474 us
    unnamed x11 -> x6, local copies, waits for them, and re-layouts: 24.2 us -> 0.01 us
    pallas_call x2 -> x3, Pallas kernels: 462 us -> 474 us  [the longest x1 255 us: gradients(): pl.pallas_call(reduce_kernel, in_specs=[vmem] * 2 + [pl.BlockSpec(memory_...]
where the time goes in v4:
time: 480 us
  Pallas kernels  474 us (99%)
  other arithmetic  4.96 us (1%)
    pallas_call x1, Pallas kernels, gradients(): pl.pallas_call(reduce_kernel, in_specs=[vmem] * 2 + [pl.BlockSpec(memory_...  255 us
    pallas_call x1, Pallas kernels, gather(): pl.pallas_call(gather_kernel, in_specs=[pl.BlockSpec(memory_space=pltpu.V...  195 us
    pallas_call x1, Pallas kernels, emit(): pl.pallas_call(emit_kernel, in_specs=[pl.BlockSpec(memory_space=pltpu.VME...  24.3 us

profile of v4, /device:TPU:2, one launch (start us, length us, event | category | flops | bytes accessed | tf_op | source)
XLA Modules:
  0.0 479.6 jit_solution(6748217075490430288)
XLA Ops:
  0.6 0.0 copy-start
  0.7 0.0 copy-start.1
  0.7 0.0 copy-start.2
  0.7 254.9 %reduce.1 = (f32[2,4,8192]{2,1,0:T(4,128)}, f32[2,4,8192]{2,1,0:T(4,128)}, f32[2,64,512]{2,1,0:T(8,128)}) custom-call(bf16[1024,512]{1,0:T(8,128)(2,1)} %bitcast.5, bf16[1024,512]{1,0:T(8,128)(2,1)} %bitcast.6, bf16[2,512,8192]{2,1,0:T(8,128)(2,1)} %wg.1, bf16[2,512,8192]{2,1,0:T(8,128)(2,1)} %wu.1, bf16[2,8192,512]{2,1,0:T(8,128)(2,1)} %wd.1), custom_call_target="tpu_custom_call" | custom-call | tf_op jit(solution)/shard_map/reduce/pallas_call | solution.py:433
  255.6 0.0 copy-done
  255.6 0.0 copy-done.1
  255.6 2.0 fusion.8
  257.5 0.0 copy-done.2
  257.5 3.0 fusion.2
  260.5 194.6 %gather.1 = (bf16[2,4,4,32,8192]{4,3,2,1,0:T(8,128)(2,1)S(1)}, bf16[2,4,4,32,8192]{4,3,2,1,0:T(8,128)(2,1)S(1)}, bf16[2,4,4,8,64,512]{5,4,3,2,1,0:T(8,128)(2,1)}) custom-call(bf16[2,4,8192]{2,1,0:T(4,128)(2,1)S(1)} %get-tuple-element.33.ng, bf16[2,4,8192]{2,1,0:T(4,128)(2,1)S(1)} %get-tuple-element.36.nu, bf16[2,64,512]{2,1,0:T(8,128)(2,1)S(1)} %get-tuple-element.27.nd), custom_call_target="tpu_custom_call" | custom-call | tf_op jit(solution)/shard_map/gather/pallas_call | solution.py:591
  455.1 24.3 %emit.1 = (bf16[2,4,4,32,8192]{4,3,2,1,0:T(8,128)(2,1)}, bf16[2,4,4,32,8192]{4,3,2,1,0:T(8,128)(2,1)}, bf16[2,4,4,8,64,512]{5,4,3,2,1,0:T(8,128)(2,1)}) custom-call(bf16[2,4,4,32,8192]{4,3,2,1,0:T(8,128)(2,1)S(1)} %get-tuple-element.21.g, bf16[2,4,4,32,8192]{4,3,2,1,0:T(8,128)(2,1)S(1)} %get-tuple-element.22.u, ...), custom_call_target="tpu_custom_call" | custom-call | tf_op jit(solution)/shard_map/emit/pallas_call | solution.py:630
Async XLA Ops:
  0.6 254.9 %copy-start = (f32[2,64,512]{2,1,0:T(8,128)S(1)}, f32[2,64,512]{2,1,0:T(8,128)}, u32[]{:S(2)}) copy-start(f32[2,64,512]{2,1,0:T(8,128)} %param.21) | copy-start | bytes 786436
  0.7 254.9 %copy-start.1 = (f32[2,64,512]{2,1,0:T(8,128)S(1)}, f32[2,64,512]{2,1,0:T(8,128)}, u32[]{:S(2)}) copy-start(f32[2,64,512]{2,1,0:T(8,128)} %param.18) | copy-start | bytes 786436
  0.7 256.9 %copy-start.2 = (f32[2,4,8192]{2,1,0:T(4,128)S(1)}, f32[2,4,8192]{2,1,0:T(4,128)}, u32[]{:S(2)}) copy-start(f32[2,4,8192]{2,1,0:T(4,128)} %param.19) | copy-start | bytes 786436

commit v5 on v4

--- a/solution.py
+++ b/solution.py
@@ -9,8 +9,11 @@
 
 GRID = (4, 4, 8)
 BF, F32 = jnp.bfloat16, jnp.float32
+ALL = Ellipsis
 MESH = pl.DeviceIdType.MESH
 VMEM_LIMIT = 66_000_000
+GATHER_LAG = 3
+EMIT_VMEM = 10 << 20
 GATHER_VMEM = 12 << 20
 LAG = 2
 SLOTS = 6
@@ -53,18 +56,19 @@
         self.n, self.p = GRID[axis], at[axis]
         self.to = (neighbour(axis, 1), neighbour(axis, -1))
         self.send, self.recv = send, recv
+        self.slots = bool(send.shape)
 
     def block(self, step):
         return lax.rem(self.p + (step + self.n), self.n)
 
     def copy(self, step, slot, d, src, dst):
         return pltpu.make_async_remote_copy(
-            src_ref=src, dst_ref=dst, send_sem=self.send.at[step, slot], recv_sem=self.recv.at[step, slot],
+            src_ref=src, dst_ref=dst, send_sem=self.send.at[step, slot] if self.slots else self.send, recv_sem=self.recv.at[step, slot],
             device_id={"dp": self.to[d]}, device_id_type=MESH,
         )
 
     def wait(self, step, slot, both):
-        for sem in (self.recv, self.send):
+        for sem in (self.recv, self.send) if self.slots else (self.recv,):
             pltpu.make_async_copy(both, both, sem.at[step, slot]).wait()
 
 
@@ -82,15 +86,15 @@
 
     def start(self):
         for block, stage, _, copy in self.copies:
-            stage[...] = self.own(block)[...].astype(BF)
+            stage[ALL] = self.own(block)[ALL].astype(BF)
             copy.start()
 
     def finish(self):
-        done = self.own(self.mine)[...]
+        done = self.own(self.mine)[ALL]
         for _, _, recv, copy in self.copies:
             copy.wait_recv()
             copy.wait_send()
-            done = done + recv[...].astype(F32)
+            done = done + recv[ALL].astype(F32)
         return done
 
 
@@ -110,10 +114,10 @@
         dgate[s] = (ct * up * (sig + silu * (1.0 - sig))).astype(BF)
 
     if layer == 1:
-        da[...] += dot(dgate[...], wg, ((1,), (1,))) + dot(dup[...], wu, ((1,), (1,)))
+        da[ALL] += dot(dgate[ALL], wg, ((1,), (1,))) + dot(dup[ALL], wu, ((1,), (1,)))
 
     at = at_all[layer]
-    return dot(at, dgate[...]), dot(at, dup[...]), dot(hid[...], dh[layer], ((0,), (0,)))
+    return dot(at, dgate[ALL]), dot(at, dup[ALL]), dot(hid[ALL], dh[layer], ((0,), (0,)))
 
 
 def reduce_kernel(x, dy, wg, wu, wd, out_g, out_u, out_d, *scratch):
@@ -152,13 +156,13 @@
             for d in (0, 1):
                 block = own(s.block(q if d == 0 else -q))
                 into = halves(array, block)[d] if j == 1 else block
-                into[...] = (into[...].astype(F32) + recv[j - 1][slot, d].astype(F32)).astype(BF)
+                into[ALL] = (into[ALL].astype(F32) + recv[j - 1][slot, d].astype(F32)).astype(BF)
                 s.copy(j, slot, d, block, recv[j].at[slot, d]).start()
 
         def last():
             j = s.n // 2
             s.wait(j - 1, slot, recv[j - 1].at[slot])
-            return own(s.p)[...].astype(F32) + recv[j - 1][slot, 0].astype(F32) + recv[j - 1][slot, 1].astype(F32)
+            return own(s.p)[ALL].astype(F32) + recv[j - 1][slot, 0].astype(F32) + recv[j - 1][slot, 1].astype(F32)
 
         return start, middle, last
 
@@ -167,7 +171,7 @@
 
         def start():
             for d, half in enumerate(halves(array, own(s.block(s.n // 2)))):
-                stage[0][slot, d] = half[...].astype(BF)
+                stage[0][slot, d] = half[ALL].astype(BF)
                 s.copy(0, slot, d, stage[0].at[slot, d], recv[0].at[slot, d]).start()
 
         def middle(j):
@@ -176,14 +180,14 @@
             for d in (0, 1):
                 block = own(s.block(q if d == 0 else -q))
                 into = halves(array, block)[d] if j == 1 else block
-                into[...] = into[...] + recv[j - 1][slot, d].astype(F32)
-                stage[j][slot, d] = block[...].astype(BF)
+                into[ALL] = into[ALL] + recv[j - 1][slot, d].astype(F32)
+                stage[j][slot, d] = block[ALL].astype(BF)
                 s.copy(j, slot, d, stage[j].at[slot, d], recv[j].at[slot, d]).start()
 
         def last():
             j = s.n // 2
             s.wait(j - 1, slot, recv[j - 1].at[slot])
-            return own(s.p)[...] + recv[j - 1][slot, 0].astype(F32) + recv[j - 1][slot, 1].astype(F32)
+            return own(s.p)[ALL] + recv[j - 1][slot, 0].astype(F32) + recv[j - 1][slot, 1].astype(F32)
 
         return start, middle, last
 
@@ -196,15 +200,15 @@
         at_all[layer] = a.T
 
     def begin():
-        enter(0, x[...])
-        dh[1] = dy[...]
-        da[...] = jnp.zeros_like(da)
+        enter(0, x[ALL])
+        dh[1] = dy[ALL]
+        da[ALL] = jnp.zeros_like(da)
 
     def between():
-        h = x[...] + da[...].astype(BF)
-        h1[...] = h
+        h = x[ALL] + da[ALL].astype(BF)
+        h1[ALL] = h
         enter(1, h)
-        da[...] = jnp.zeros_like(da)
+        da[ALL] = jnp.zeros_like(da)
 
     def weights(i, act):
         slot, layer = lax.rem(i, 2), lax.rem(lax.div(i, chunks), 2)
@@ -349,10 +353,10 @@
         at_stage(4, ny, "last")(lambda c: w_direct().start())
 
     def backward_norm():
-        h, by_a = h1[...].astype(F32), da[...].astype(BF).astype(F32)
+        h, by_a = h1[ALL].astype(F32), da[ALL].astype(BF).astype(F32)
         scale = lax.rsqrt(jnp.mean(h**2, -1, keepdims=True) + 1e-6)
         by_h = scale * by_a - h * (scale**3 * jnp.mean(by_a * h, -1, keepdims=True))
-        dh[0] = dy[...] + by_h.astype(BF)
+        dh[0] = dy[ALL] + by_h.astype(BF)
 
     def produce(layer, c):
         slot, long = lax.rem(c, SLOTS), lax.rem(c, 2 * SLOTS)
@@ -443,14 +447,30 @@
     )(x, dy, wg, wu, wd)
 
 
-def gather_kernel(ng, nu, nd, og, ou, od, *scratch):
-    zb, yg, yu, local, sems = scratch
+def gather_kernel(sums, m, v, weights, og, ou, od, *scratch):
+    ng, nu, nd, rows_gu, rows_d, sums_held, m_held, v_held, zb, yg, yu, local, rows_sem, held_sem, sems = scratch
     nx, ny, nz = GRID
     total = 2 * JOBS
     f, r = zb.shape[-1], nd.shape[1] // JOBS
     at, neighbour = place()
     x_, y_, z_ = at
     met = greet(neighbour, False)
+    me = lax.axis_index("dp")
+    rg, rd = ng.shape[1], nd.shape[1]
+    eight = pl.ds(pl.multiple_of(lax.div(me, 8 // rg) * 8, 8), 8)
+    own = [pltpu.make_async_copy(w.at[:, eight], rows_gu.at[k], rows_sem.at[k]) for k, w in enumerate(weights[:2])]
+    own.append(pltpu.make_async_copy(weights[2].at[:, pl.ds(pl.multiple_of(me * rd, rd), rd)], rows_d, rows_sem.at[2]))
+    for i, (a, b) in enumerate(((sums, sums_held), (m, m_held), (v, v_held))):
+        own += [pltpu.make_async_copy(a[k], b[k], held_sem.at[i, k]) for k in range(3)]
+    for c in own:
+        c.start()
+    for c in own:
+        c.wait()
+    upper = lax.rem(me, 8 // rg) == 1
+    for k, new in enumerate((ng, nu)):
+        w = jnp.where(upper, rows_gu[k, :, rg:].astype(F32), rows_gu[k, :, :rg].astype(F32))
+        new[ALL] = adamw(w, m_held[k][ALL], v_held[k][ALL], sums_held[k][ALL])[0]
+    nd[ALL] = adamw(rows_d[ALL].astype(F32), m_held[2][ALL], v_held[2][ALL], sums_held[2][ALL])[0]
     names = (("w1", 2), ("g2", 1), ("g3", 0), ("u2", 0), ("u3", 1), ("d1", 0), ("d2", 1), ("d3", 2))
     odd = (("e1", 1), ("e2", 0), ("e3", 2))
     senders = {name: Sender(axis, at, neighbour, *sem) for (name, axis), sem in zip((*names, *odd), (*sems, *sems[5:]), strict=True)}
@@ -489,20 +509,20 @@
         for d in (0, 1):
             b = s.block(-i if d == 0 else i)
             dst = full(b) if i < s.n // 2 - 1 else half(b)[d]
-            s.copy(i, lax.rem(j, SLOTS), d, first if first is not None else dst, dst).start()
+            s.copy(i, j, d, first if first is not None else dst, dst).start()
 
     def arrived(name, j, i):
         s = senders[name]
         full = blocks(name, j)[0]
-        s.wait(i, lax.rem(j, SLOTS), full(pl.ds(0, 2) if i < s.n // 2 - 1 else 0))
+        s.wait(i, j, full(pl.ds(0, 2) if i < s.n // 2 - 1 else 0))
 
     def tick(t, carry):
         def at_stage(k, fn):
-            j = t - LAG * k
+            j = t - GATHER_LAG * k
             pl.when((j >= 0) & (j < total))(lambda: fn(j))
 
         def keep(which, j):
-            slot = lax.rem(j, SLOTS)
+            slot = j
             src, name, b = ((yg, "g2", y_), (yu, "u2", x_))[which]
             return pltpu.make_async_copy(src.at[slot], blocks(name, j)[0](b), local.at[which, slot])
 
@@ -513,7 +533,7 @@
             ring("w1", j, 0)
 
         def turn(j):
-            slot = lax.rem(j, SLOTS)
+            slot = j
             arrived("w1", j, nz // 2 - 1)
             for which, (yb, name) in enumerate(((yg, "g2"), (yu, "u2"))):
                 yb[slot] = zb[j, :, which].reshape(yb.shape[1:])
@@ -546,7 +566,7 @@
         def own_rows(name, j):
             layer, q = piece(j)
             own = nd.at[layer, pl.ds(pl.multiple_of(q * r, r), r)]
-            return own, pltpu.make_async_copy(own, blocks(name + "1", j)[0](x_ if name == "d" else y_), local.at[2, lax.rem(j, SLOTS)])
+            return own, pltpu.make_async_copy(own, blocks(name + "1", j)[0](x_ if name == "d" else y_), local.at[2, j])
 
         def d_begin(name, j):
             own, copy = own_rows(name, j)
@@ -577,86 +597,100 @@
         return carry
 
     pl.semaphore_wait(pltpu.get_barrier_semaphore(), met)
-    lax.fori_loop(0, total + LAG * (nz // 2 + 4), tick, 0)
-
-
-def gather(ng, nu, nd):
+    lax.fori_loop(0, total + GATHER_LAG * (nz // 2 + 4), tick, 0)
+    xs, ys, zs = (pl.ds(0, n - 1) for n in GRID)
+    sent = (zb.at[:, zs], og.at[:, xs, 0], og.at[:, xs], ou.at[:, ys, 0], ou.at[:, :, ys], od.at[:, xs, 0, 0], od.at[:, :, ys, 0], od.at[:, :, :, zs])
+    for (send, _), what in zip(sems, sent, strict=True):
+        pltpu.make_async_copy(what, what, send).wait()
+
+
+def gather(sums, m, v, weights):
     nx, ny, nz = GRID
-    _, rg, ff = ng.shape
-    _, rd, d = nd.shape
+    _, rg, ff = sums[0].shape
+    _, rd, d = sums[2].shape
+    hbm = [pl.BlockSpec(memory_space=pltpu.HBM)] * 3
+    held = [pltpu.VMEM(a.shape, F32) for a in m]
     f, jobs = ff // JOBS, 2 * JOBS
     dma = pltpu.SemaphoreType.DMA
     steps = (nz, ny, nx, nx, ny, nx, ny, nz)
     wide = jax.ShapeDtypeStruct((2, nx, ny, nz * rg, ff), BF)
-    got = pl.pallas_call(
+    return pl.pallas_call(
         gather_kernel,
-        in_specs=[pl.BlockSpec(memory_space=pltpu.VMEM)] * 3,
+        in_specs=[hbm] * 4,
         out_specs=[pl.BlockSpec(memory_space=pl.ANY)] * 3,
         out_shape=[wide, wide, jax.ShapeDtypeStruct((2, nx, ny, nz, rd, d), BF)],
         scratch_shapes=[
-            pltpu.VMEM((jobs, nz, 2, rg, f), BF), pltpu.VMEM((SLOTS, nz * rg, f), BF), pltpu.VMEM((SLOTS, nz * rg, f), BF),
-            dma((3, SLOTS)),
-            [(dma((n // 2, SLOTS)), dma((n // 2, SLOTS))) for n in steps],
+            pltpu.VMEM((2, rg, ff), BF), pltpu.VMEM((2, rg, ff), BF), pltpu.VMEM((2, rd, d), BF),
+            pltpu.VMEM((2, 2, 8, ff), BF), pltpu.VMEM((2, rd, d), BF), held, held, held,
+            pltpu.VMEM((jobs, nz, 2, rg, f), BF), pltpu.VMEM((jobs, nz * rg, f), BF), pltpu.VMEM((jobs, nz * rg, f), BF),
+            dma((3, jobs)), dma((3,)), dma((3, 3)),
+            [(dma, dma((n // 2, jobs))) for n in steps],
         ],
         compiler_params=pltpu.CompilerParams(vmem_limit_bytes=GATHER_VMEM, collective_id=1, has_side_effects=True),
         name="gather",
-    )(ng, nu, nd)
-    og, ou, od = emit(*got)
-    n = nx * ny * nz
-    return og.reshape(2, n * rg, ff), ou.reshape(2, n * rg, ff), od.reshape(2, n * rd, d)
-
-
-def emit_kernel(g, u, d, go, uo, do, hold, sems):
+    )(sums, m, v, weights)
+
+
+def emit_kernel(gathered, sums, m, v, outs, new_m, new_v, hold, sums_held, m_held, v_held, sems, small_sems):
+    g, u, d = gathered
+    go, uo, do = outs
     copies = [pltpu.make_async_copy(a.at[i], b.at[i], sems.at[k, i]) for k, (a, b) in enumerate(((g, go), (u, uo))) for i in range(2)]
-    for c in copies:
+    parts = [(i, x) for i in range(2) for x in range(d.shape[1])]
+    slots = hold.shape[0]
+    ins = [pltpu.make_async_copy(d.at[p], hold.at[k % slots], sems.at[2, k]) for k, p in enumerate(parts)]
+    writes = [pltpu.make_async_copy(hold.at[k % slots], do.at[p], sems.at[3, k]) for k, p in enumerate(parts)]
+    small = [pltpu.make_async_copy(a[k], b[k], small_sems.at[i, k]) for i, (a, b) in enumerate(((sums, sums_held), (m, m_held), (v, v_held))) for k in range(3)]
+    back = [pltpu.make_async_copy(a[k], b[k], small_sems.at[3 + i, k]) for i, (a, b) in enumerate(((m_held, new_m), (v_held, new_v))) for k in range(3)]
+    for c in small + ins[:slots] + copies:
         c.start()
-    pieces = [(i, x) for i in range(2) for x in range(4)]
-    slots = hold.shape[0]
-    ins = [pltpu.make_async_copy(d.at[p], hold.at[k % slots], sems.at[2, k]) for k, p in enumerate(pieces)]
-    outs = [pltpu.make_async_copy(hold.at[k % slots], do.at[p], sems.at[3, k]) for k, p in enumerate(pieces)]
-    for c in ins[:slots]:
+    for c in small:
+        c.wait()
+    for k in range(3):
+        _, m_held[k][ALL], v_held[k][ALL] = adamw(None, m_held[k][ALL], v_held[k][ALL], sums_held[k][ALL])
+    for c in back:
         c.start()
-    for k in range(len(pieces)):
+    for k in range(len(parts)):
         ins[k].wait()
-        outs[k].start()
-        if k >= 1 and k - 1 + slots < len(pieces):
-            outs[k - 1].wait()
+        writes[k].start()
+        if k >= 1 and k - 1 + slots < len(parts):
+            writes[k - 1].wait()
             ins[k - 1 + slots].start()
-    for c in outs[len(pieces) - slots:] + copies:
+    for c in writes[len(parts) - slots:] + copies + back:
         c.wait()
 
 
-def emit(*arrays):
-    return pl.pallas_call(
+def emit(gathered, sums, m, v):
+    vmem, hbm = pl.BlockSpec(memory_space=pltpu.VMEM), pl.BlockSpec(memory_space=pltpu.HBM)
+    dma = pltpu.SemaphoreType.DMA
+    moments = [jax.ShapeDtypeStruct(a.shape, F32) for a in m]
+    held = [pltpu.VMEM(a.shape, F32) for a in m]
+    outs, new_m, new_v = pl.pallas_call(
         emit_kernel,
-        in_specs=[pl.BlockSpec(memory_space=pltpu.VMEM), pl.BlockSpec(memory_space=pltpu.VMEM), pl.BlockSpec(memory_space=pltpu.HBM)],
-        out_specs=[pl.BlockSpec(memory_space=pltpu.HBM)] * 3,
-        out_shape=[jax.ShapeDtypeStruct(a.shape, BF) for a in arrays],
-        scratch_shapes=[pltpu.VMEM((3, *arrays[2].shape[2:]), BF), pltpu.SemaphoreType.DMA((4, 8))],
-        compiler_params=pltpu.CompilerParams(vmem_limit_bytes=7 << 20),
+        in_specs=[[vmem, vmem, hbm], [hbm] * 3, [hbm] * 3, [hbm] * 3],
+        out_specs=[[hbm] * 3, [hbm] * 3, [hbm] * 3],
+        out_shape=[[jax.ShapeDtypeStruct(a.shape, BF) for a in gathered], moments, moments],
+        scratch_shapes=[pltpu.VMEM((3, *gathered[2].shape[2:]), BF), held, held, held, dma((4, 8)), dma((5, 3))],
+        compiler_params=pltpu.CompilerParams(vmem_limit_bytes=EMIT_VMEM),
         name="emit",
-    )(*arrays)
+    )(gathered, sums, m, v)
+    return (*(a.reshape(2, -1, w.shape[2]) for a, w in zip(outs, m, strict=True)), *new_m, *new_v)
 
 
 def adamw(w, m, v, g):
-    g = lax.reduce_precision(g, 8, 7)
+    g = g.astype(BF).astype(F32)
     m = 0.9 * m + 0.1 * g
     v = 0.95 * v + 0.05 * g * g
+    if w is None:
+        return None, m, v
     step = m * lax.rsqrt(v + 1e-8) + 0.1 * w
     return (w - 0.02 * step).astype(BF), m, v
 
 
 def device_step(x, dy, *arrays):
-    weights, ms, vs = (arrays[i:i + 3] for i in (0, 3, 6))
+    weights, m, v = (list(arrays[i:i + 3]) for i in (0, 3, 6))
     sums = gradients(x[0], dy[0], *weights)
-    me = lax.axis_index("dp")
-    new = []
-    for w, m, v, g in zip(weights, ms, vs, sums, strict=True):
-        rows = m.shape[1]
-        own = lax.dynamic_slice_in_dim(w, me * rows, rows, 1).astype(F32)
-        new.append(adamw(own, m, v, g))
-    gathered = gather(*(one[0] for one in new))
-    return (*gathered, *(one[1] for one in new), *(one[2] for one in new))
+    sums, m, v = ([pltpu.with_memory_space_constraint(t, pltpu.HBM) for t in ts] for ts in (sums, m, v))
+    return emit(list(gather(sums, m, v, weights)), sums, m, v)
 
 
 def solution(mesh):

time: 480 us -> 475 us (0.990)
  other arithmetic: 4.96 us -> 0 us
    convert_element_type x2 -> x0, other arithmetic: 4.96 us -> none  [adamw(): return ((w - 0.02 * step).astype(BF), m, v)]
where the time goes in v5:
time: 475 us
  Pallas kernels  474 us (100%)
    pallas_call x1, Pallas kernels, gradients(): pl.pallas_call(reduce_kernel, in_specs=[vmem] * 2 + [pl.BlockSpec(memory_...  255 us
    pallas_call x1, Pallas kernels, gather(): pl.pallas_call(gather_kernel, in_specs=[hbm] * 4, out_specs=[pl.BlockSpec...  194 us
    pallas_call x1, Pallas kernels, emit(): pl.pallas_call(emit_kernel, in_specs=[[vmem, vmem, hbm], [hbm] * 3, [hbm]...  25.8 us

profile of v5, /device:TPU:2, one launch (start us, length us, event | category | flops | bytes accessed | tf_op | source)
XLA Modules:
  0.0 475.0 jit_solution(7545212317971933398)
XLA Ops:
  0.6 254.8 %reduce.1 = (f32[2,4,8192]{2,1,0:T(4,128)}, f32[2,4,8192]{2,1,0:T(4,128)}, f32[2,64,512]{2,1,0:T(8,128)}) custom-call(bf16[1024,512]{1,0:T(8,128)(2,1)} %bitcast.5, bf16[1024,512]{1,0:T(8,128)(2,1)} %bitcast.6, bf16[2,512,8192]{2,1,0:T(8,128)(2,1)} %weights_0_.1, bf16[2,512,8192]{2,1,0:T(8,128)(2,1)} %weights_1_.1, bf16[2,8192,512]{2,1,0:T(8,128)(2,1)} %weights_2_.1), custom_call_target="tpu_custom_call" | custom-call | tf_op jit(solution)/shard_map/reduce/pallas_call | solution.py:437
  255.5 193.6 %gather.1 = (bf16[2,4,4,32,8192]{4,3,2,1,0:T(8,128)(2,1)S(1)}, bf16[2,4,4,32,8192]{4,3,2,1,0:T(8,128)(2,1)S(1)}, bf16[2,4,4,8,64,512]{5,4,3,2,1,0:T(8,128)(2,1)}) custom-call(f32[2,4,8192]{2,1,0:T(4,128)} %get-tuple-element.24.sums_0_, f32[2,4,8192]{2,1,0:T(4,128)} %get-tuple-element.25.sums_1_, f32[2,64,512]{2,1,0:T(8,128)} %get-tuple-element.26.sums_2_, ...), custom_call_target="tpu_custom_call" | custom-call | tf_op jit(solution)/shard_map/gather/pallas_call | solution.py:617
  449.1 25.8 %emit.1 = (bf16[2,4,4,32,8192]{4,3,2,1,0:T(8,128)(2,1)}, bf16[2,4,4,32,8192]{4,3,2,1,0:T(8,128)(2,1)}, bf16[2,4,4,8,64,512]{5,4,3,2,1,0:T(8,128)(2,1)}, f32[2,4,...) custom-call(bf16[2,4,4,32,8192]{4,3,2,1,0:T(8,128)(2,1)S(1)} %get-tu, ...), custom_call_target="tpu_custom_call" | custom-call | tf_op jit(solution)/shard_map/emit/pallas_call | solution.py:667

commit v6 on v5

--- a/solution.py
+++ b/solution.py
@@ -12,7 +12,7 @@
 ALL = Ellipsis
 MESH = pl.DeviceIdType.MESH
 VMEM_LIMIT = 66_000_000
-GATHER_LAG = 3
+GATHER_LAG = 4
 EMIT_VMEM = 10 << 20
 GATHER_VMEM = 12 << 20
 LAG = 2
@@ -120,8 +120,8 @@
     return dot(at, dgate[ALL]), dot(at, dup[ALL]), dot(hid[ALL], dh[layer], ((0,), (0,)))
 
 
-def reduce_kernel(x, dy, wg, wu, wd, out_g, out_u, out_d, *scratch):
-    (hid, dgate, dup, da, dh, a_all, at_all, h1,
+def reduce_kernel(x_in, dy_in, wg, wu, wd, out_g, out_u, out_d, *scratch):
+    (x, in_sem, hid, dgate, dup, da, dh, a_all, at_all, h1,
      own_g, own_u, own_d, acc_g2, acc_u2, acc_w3, acc_d2, acc_d3,
      rg, ru, rw, rd, sg, su, sw, sd, sems, direct, hold_g, hold_u, hold_d, hold_sem) = scratch
     nx, ny, nz = GRID
@@ -199,12 +199,15 @@
         a_all[layer] = a
         at_all[layer] = a.T
 
+    loads = [pltpu.make_async_copy(a, b, in_sem.at[k]) for k, (a, b) in enumerate(((x_in, x), (dy_in, dh.at[1])))]
+
     def begin():
+        loads[0].wait()
         enter(0, x[ALL])
-        dh[1] = dy[ALL]
         da[ALL] = jnp.zeros_like(da)
 
     def between():
+        loads[1].wait()
         h = x[ALL] + da[ALL].astype(BF)
         h1[ALL] = h
         enter(1, h)
@@ -356,7 +359,7 @@
         h, by_a = h1[ALL].astype(F32), da[ALL].astype(BF).astype(F32)
         scale = lax.rsqrt(jnp.mean(h**2, -1, keepdims=True) + 1e-6)
         by_h = scale * by_a - h * (scale**3 * jnp.mean(by_a * h, -1, keepdims=True))
-        dh[0] = dy[ALL] + by_h.astype(BF)
+        dh[0] = dh[1] + by_h.astype(BF)
 
     def produce(layer, c):
         slot, long = lax.rem(c, SLOTS), lax.rem(c, 2 * SLOTS)
@@ -376,6 +379,8 @@
 
         lax.fori_loop(start, stop, tick, 0)
 
+    for c in loads:
+        c.start()
     weights(0, lambda c: c.start())
     met = greet(neighbour, True)
     begin()
@@ -411,6 +416,7 @@
         return (dma((n // 2, count)), dma((n // 2, count)))
 
     scratch = [
+        pltpu.VMEM((tokens, d), BF), dma((2,)),
         pltpu.VMEM((tokens, f), BF), pltpu.VMEM((tokens, f), BF), pltpu.VMEM((tokens, f), BF),
         pltpu.VMEM((tokens, d), F32), pltpu.VMEM((2, tokens, d), BF),
         pltpu.VMEM((2, tokens, d), BF), pltpu.VMEM((2, d, tokens), BF), pltpu.VMEM((tokens, d), BF),
@@ -436,7 +442,7 @@
     vmem = pl.BlockSpec(memory_space=pltpu.VMEM)
     return pl.pallas_call(
         reduce_kernel,
-        in_specs=[vmem] * 2 + [pl.BlockSpec(memory_space=pl.ANY)] * 3,
+        in_specs=[pl.BlockSpec(memory_space=pl.ANY)] * 5,
         out_specs=[vmem] * 3,
         out_shape=[jax.ShapeDtypeStruct((2, rg, ff), F32)] * 2 + [jax.ShapeDtypeStruct((2, rd, d), F32)],
         scratch_shapes=scratch,
@@ -641,20 +647,22 @@
     writes = [pltpu.make_async_copy(hold.at[k % slots], do.at[p], sems.at[3, k]) for k, p in enumerate(parts)]
     small = [pltpu.make_async_copy(a[k], b[k], small_sems.at[i, k]) for i, (a, b) in enumerate(((sums, sums_held), (m, m_held), (v, v_held))) for k in range(3)]
     back = [pltpu.make_async_copy(a[k], b[k], small_sems.at[3 + i, k]) for i, (a, b) in enumerate(((m_held, new_m), (v_held, new_v))) for k in range(3)]
-    for c in small + ins[:slots] + copies:
-        c.start()
-    for c in small:
-        c.wait()
-    for k in range(3):
-        _, m_held[k][ALL], v_held[k][ALL] = adamw(None, m_held[k][ALL], v_held[k][ALL], sums_held[k][ALL])
-    for c in back:
+    for c in ins[:slots] + copies + small:
         c.start()
     for k in range(len(parts)):
+        if k == slots:
+            for c in small:
+                c.wait()
+            for mk, vk, sk in zip(m_held, v_held, sums_held, strict=True):
+                _, mk[ALL], vk[ALL] = adamw(None, mk[ALL], vk[ALL], sk[ALL])
         ins[k].wait()
         writes[k].start()
         if k >= 1 and k - 1 + slots < len(parts):
             writes[k - 1].wait()
             ins[k - 1 + slots].start()
+        if k == slots:
+            for c in back:
+                c.start()
     for c in writes[len(parts) - slots:] + copies + back:
         c.wait()
 

time: 475 us -> 475 us (level)
  no operation moved by 1% of the time
where the time goes in v6:
time: 475 us
  Pallas kernels  474 us (100%)
    pallas_call x1, Pallas kernels, gradients(): pl.pallas_call(reduce_kernel, in_specs=[pl.BlockSpec(memory_space=pl.ANY)...  254 us
    pallas_call x1, Pallas kernels, gather(): pl.pallas_call(gather_kernel, in_specs=[hbm] * 4, out_specs=[pl.BlockSpec...  195 us
    pallas_call x1, Pallas kernels, emit(): pl.pallas_call(emit_kernel, in_specs=[[vmem, vmem, hbm], [hbm] * 3, [hbm]...  25.4 us

profile of v6, /device:TPU:2, one launch (start us, length us, event | category | flops | bytes accessed | tf_op | source)
XLA Modules:
  0.0 475.0 jit_solution(12439281621440193982)
XLA Ops:
  0.6 254.1 %reduce.1 = (f32[2,4,8192]{2,1,0:T(4,128)}, f32[2,4,8192]{2,1,0:T(4,128)}, f32[2,64,512]{2,1,0:T(8,128)}) custom-call(bf16[1024,512]{1,0:T(8,128)(2,1)} %bitcast.5, bf16[1024,512]{1,0:T(8,128)(2,1)} %bitcast.6, bf16[2,512,8192]{2,1,0:T(8,128)(2,1)} %weights_0_.1, bf16[2,512,8192]{2,1,0:T(8,128)(2,1)} %weights_1_.1, bf16[2,8192,512]{2,1,0:T(8,128)(2,1)} %weights_2_.1), custom_call_target="tpu_custom_call" | custom-call | tf_op jit(solution)/shard_map/reduce/pallas_call | solution.py:443
  254.8 194.7 %gather.1 = (bf16[2,4,4,32,8192]{4,3,2,1,0:T(8,128)(2,1)S(1)}, bf16[2,4,4,32,8192]{4,3,2,1,0:T(8,128)(2,1)S(1)}, bf16[2,4,4,8,64,512]{5,4,3,2,1,0:T(8,128)(2,1)}) custom-call(f32[2,4,8192]{2,1,0:T(4,128)} %get-tuple-element.24.sums_0_, f32[2,4,8192]{2,1,0:T(4,128)} %get-tuple-element.25.sums_1_, f32[2,64,512]{2,1,0:T(8,128)} %get-tuple-element.26.sums_2_, ...), custom_call_target="tpu_custom_call" | custom-call | tf_op jit(solution)/shard_map/gather/pallas_call | solution.py:623
  449.4 25.4 %emit.1 = (bf16[2,4,4,32,8192]{4,3,2,1,0:T(8,128)(2,1)}, bf16[2,4,4,32,8192]{4,3,2,1,0:T(8,128)(2,1)}, bf16[2,4,4,8,64,512]{5,4,3,2,1,0:T(8,128)(2,1)}, f32[2,4,...) custom-call(bf16[2,4,4,32,8192]{4,3,2,1,0:T(8,128)(2,1)S(1)} %get-tu, ...), custom_call_target="tpu_custom_call" | custom-call | tf_op jit(solution)/shard_map/emit/pallas_call | solution.py:675
